TPU v7x, 8 devices: a whole 2x2x1 slice. The times are simulated.
8 devices in a mesh: dp: 2 (over z, y), tp: 4 (over x, core).
Axes of the slice: x: 2, y: 2, z: 1, core: 2. Of those that a mesh axis runs over, the one named last changes fastest.
Arguments:
- x_in: bfloat16 [2, 128, 2560], P('dp', 'tp'), parts along dimension 0
- y_grad: bfloat16 [2, 128, 2560], P('dp', 'tp'), parts along dimension 0
- ln_par: float32 [2, 4, 2560], replicated
- bias_d: float32 [2, 2, 2560], replicated
- w_qkv: bfloat16 [2, 2560, 3, 20, 128], P(None, None, None, 'tp')
- w_out: bfloat16 [2, 20, 128, 2560], P(None, 'tp')
- w_up: bfloat16 [2, 2560, 10240], P(None, None, 'tp')
- b_up: float32 [2, 10240], P(None, 'tp')
- w_down: bfloat16 [2, 10240, 2560], P(None, 'tp')
Outputs:
- output 1: bfloat16 [2, 128, 2560], P('dp', 'tp'), parts along dimension 0
- output 2: bfloat16 [2, 128, 2560], P('dp', 'tp'), parts along dimension 0
- output 3: float32 [4, 4, 2560], P('dp'), parts along dimension 0
- output 4: float32 [4, 2, 2560], P('dp'), parts along dimension 0
- output 5: bfloat16 [4, 2560, 3, 20, 128], P('dp', None, None, 'tp'), parts along dimension 0
- output 6: bfloat16 [4, 20, 128, 2560], P('dp', 'tp'), parts along dimension 0
- output 7: bfloat16 [4, 2560, 10240], P('dp', None, 'tp'), parts along dimension 0
- output 8: float32 [4, 10240], P('dp', 'tp'), parts along dimension 0
- output 9: bfloat16 [4, 10240, 2560], P('dp', 'tp'), parts along dimension 0
There are 2 independent parts. A program takes and returns all parts, laid end to end along the dimension named above; an argument that names none is the same for every part.
All inputs are finite; a program needn't handle non-finite values.
Results may differ from a plain program's by a relative error of at most 0.02.
Values are sent between devices in bfloat16 or wider.
A program may use at most 1 GiB of HBM per device.

v0:
```python
import jax
import jax.numpy as jnp
from jax import lax
from jax.experimental import pallas as pl
from jax.experimental.pallas import tpu as pltpu
from jax.sharding import PartitionSpec as P

MESH = pl.DeviceIdType.MESH
F32, BF16 = jnp.float32, jnp.bfloat16
N_LAYERS, SEQ, BLK, D, HEADS, HD, FF = 2, 128, 32, 2560, 5, 128, 2560
ATT = HEADS * HD
QKV = 3 * ATT
C = 512
NC = D // C
SCALE = HD ** -0.5
GELU_K = 0.7978845608028654
GELU_C = 0.044715
VMEM_ALL = 67043328


def mm(a, b):
    return jnp.dot(a, b, preferred_element_type=F32)


def mm_nt(a, b):
    return lax.dot_general(a, b, (((1,), (1,)), ((), ())), preferred_element_type=F32)


def mm_tn(a, b):
    return mm(a.T, b)


def chunk(c, size=C):
    return pl.ds(pl.multiple_of(c * size, size), size)


def chain_kernel(x_ref, dy_ref, ln_ref, bias_ref, bup_ref, wqkv_h, wo_h, wu_h, wd_h,
                 y_ref, xg_ref, small_ref, bupg_ref, h_o, h2_o, dm_o, da_o, a_o, act_o, dpre_o, dqkv_o,
                 wq, wo, wu, wd, h_g, h2_g, dm_g, da_g, qkv, prob, attn, act, gp, dpre, dqkv,
                 xh1, xh2, rs1, rs2, res, acc, acct, part, own, rr, xx, ss, sg, sgr,
                 wsem, osem, agsem, rssem, gsem):
    me = lax.axis_index('tp')
    x_id = lax.div(me, 2)
    core = lax.rem(me, 2)
    sib = x_id * 2 + (1 - core)
    cross = (1 - x_id) * 2 + core
    diag = (1 - x_id) * 2 + (1 - core)

    def remote(src, dst, send, recv, dev):
        return pltpu.make_async_remote_copy(src_ref=src, dst_ref=dst, send_sem=send, recv_sem=recv,
                                            device_id={'tp': dev}, device_id_type=MESH)

    def weight_copies(kind, layer):
        if kind == 0:
            return [pltpu.make_async_copy(wqkv_h.at[layer, j], wq.at[:, pl.ds(j * HD, HD)], wsem.at[0, j]) for j in range(3 * HEADS)]
        if kind == 1:
            return [pltpu.make_async_copy(wo_h.at[layer], wo, wsem.at[1, 0])]
        src, dst = ((wu_h, wu), (wd_h, wd))[kind - 2]
        return [pltpu.make_async_copy(src.at[layer, pl.ds(j * C, C)], dst.at[pl.ds(j * C, C)], wsem.at[kind, j]) for j in range(NC)]

    def load_w(kind, layer):
        for copy in weight_copies(kind, layer):
            copy.start()

    def wait_w(kind, layer):
        for copy in weight_copies(kind, layer):
            copy.wait()

    def out_copy(i, src, dst, layer):
        return pltpu.make_async_copy(src.at[layer], dst.at[layer], osem.at[i, layer])

    outs = [(h_g, h_o), (h2_g, h2_o), (dm_g, dm_o), (da_g, da_o), (attn, a_o), (act, act_o), (dpre, dpre_o), (dqkv, dqkv_o)]

    def ag_side(g, layer, c):
        mine = g.at[layer, me, :, chunk(c)]
        return remote(mine, mine, agsem.at[0, c], agsem.at[1, c], sib)

    def ag_across(g, layer, c):
        mine = g.at[layer, me, :, chunk(c)]
        return remote(mine, mine, agsem.at[2, c], agsem.at[3, c], cross)

    def ag_forward(g, layer, c):
        theirs = g.at[layer, cross, :, chunk(c)]
        return remote(theirs, theirs, agsem.at[4, c], agsem.at[5, c], sib)

    def ag_start(g, layer):
        for c in range(NC):
            ag_across(g, layer, c).start()
        for c in range(NC):
            ag_side(g, layer, c).start()

    def ag_consume(g, layer, compute):
        @pl.loop(0, NC + 1)
        def _(c):
            @pl.when(c < NC)
            def _():
                ag_across(g, layer, c).wait_recv()
                ag_forward(g, layer, c).start()

            @pl.when(c >= 1)
            def _():
                cc = c - 1
                ag_side(g, layer, cc).wait_recv()
                ag_forward(g, layer, cc).wait_recv()
                compute(cc)

        @pl.loop(0, NC)
        def _(c):
            ag_side(g, layer, c).wait_send()
            ag_across(g, layer, c).wait_send()
            ag_forward(g, layer, c).wait_send()

    def rs_side(par, c):
        return remote(part.at[:, 1 - core, :, chunk(c)], rr.at[par, :, :, chunk(c)], rssem.at[par, 0, c], rssem.at[par, 1, c], sib)

    def rs_across(par, c):
        return remote(ss.at[:, chunk(c)], xx.at[par, :, chunk(c)], rssem.at[par, 2, c], rssem.at[par, 3, c], cross)

    def rs_run(par, compute, lag=2):
        @pl.loop(0, NC + lag)
        def _(c):
            @pl.when(c < NC)
            def _():
                vals = compute(c)
                for b in range(4):
                    part[b // 2, b % 2, :, chunk(c)] = vals[b * BLK:(b + 1) * BLK]
                rs_side(par, c).start()

            @pl.when(c >= lag)
            def _():
                cc = c - lag
                rs_side(par, cc).wait_recv()
                cols = chunk(cc)
                ss[:, cols] = (part[1 - x_id, core, :, cols] + rr[par, 1 - x_id, :, cols]).astype(BF16)
                rs_across(par, cc).start()
                own[:, cols] = part[x_id, core, :, cols] + rr[par, x_id, :, cols]

        @pl.loop(0, NC)
        def _(c):
            rs_across(par, c).wait_recv()
            rs_side(par, c).wait_send()
            rs_across(par, c).wait_send()
            own[:, chunk(c)] += xx[par, :, chunk(c)].astype(F32)

    def normed(vals, gain, shift, xh, rs, layer):
        mean_val = jnp.mean(vals, axis=-1, keepdims=True)
        centered = vals - mean_val
        rstd = lax.rsqrt(jnp.mean(centered * centered, axis=-1, keepdims=True) + 1e-5)
        hat = centered * rstd
        xh[layer] = hat
        rs[layer] = jnp.broadcast_to(rstd, (BLK, 128))
        return (hat * gain + shift).astype(BF16)

    def norm_grad(d_out, gain, xh, rs, layer, gain_row):
        hat = xh[layer]
        rstd = rs[layer][:, :1]
        sg[layer, gain_row:gain_row + 1, :] = jnp.sum(d_out * hat, axis=0, keepdims=True)
        sg[layer, gain_row + 1:gain_row + 2, :] = jnp.sum(d_out, axis=0, keepdims=True)
        d_hat = d_out * gain
        m1 = jnp.mean(d_hat, axis=-1, keepdims=True)
        m2 = jnp.mean(d_hat * hat, axis=-1, keepdims=True)
        return rstd * (d_hat - m1 - hat * m2)

    def small_copies(layer):
        return [remote(sg.at[layer], sgr.at[layer, i], gsem.at[layer, 0, i], gsem.at[layer, 1, i], dev)
                for i, dev in enumerate((sib, cross, diag))]

    load_w(0, 0)
    barrier = pltpu.get_barrier_semaphore()
    for dev in (sib, cross, diag):
        pl.semaphore_signal(barrier, inc=1, device_id={'tp': dev}, device_id_type=MESH)
    res[...] = x_ref[0].astype(F32)
    pl.semaphore_wait(barrier, 3)

    row_id = lax.broadcasted_iota(jnp.int32, (SEQ, SEQ), 0)
    col_id = lax.broadcasted_iota(jnp.int32, (SEQ, SEQ), 1)
    causal = row_id >= col_id

    @pl.loop(0, N_LAYERS)
    def _(layer):
        first = layer == 0
        lnp = ln_ref[layer]
        h_g[layer, me] = normed(res[...], lnp[0:1], lnp[1:2], xh1, rs1, layer)
        ag_start(h_g, layer)
        acc[...] = jnp.zeros_like(acc)
        wait_w(0, layer)

        @pl.when(first)
        def _():
            load_w(1, 0)
            load_w(2, 0)

        def qkv_chunk(c):
            h = h_g[layer, :, :, chunk(c)].reshape(SEQ, C)
            for n in range(0, QKV, 640):
                acc[:, n:n + 640] += mm(h, wq[chunk(c), n:n + 640])
        ag_consume(h_g, layer, qkv_chunk)
        out_copy(0, h_g, h_o, layer).start()

        @pl.when(first)
        def _():
            load_w(0, 1)

        for j in range(3 * HEADS):
            qkv[layer, :, j * HD:(j + 1) * HD] = acc[:, j * HD:(j + 1) * HD].astype(BF16)
        for hd in range(HEADS):
            q = qkv[layer, :, hd * HD:(hd + 1) * HD]
            k = qkv[layer, :, ATT + hd * HD:ATT + (hd + 1) * HD]
            v = qkv[layer, :, 2 * ATT + hd * HD:2 * ATT + (hd + 1) * HD]
            scores = jnp.where(causal, mm_nt(q, k) * SCALE, -1e30)
            e = jnp.exp(scores - jnp.max(scores, axis=-1, keepdims=True))
            p = (e / jnp.sum(e, axis=-1, keepdims=True)).astype(BF16)
            prob[layer, hd] = p
            attn[layer, :, hd * HD:(hd + 1) * HD] = mm(p, v).astype(BF16)
        out_copy(4, attn, a_o, layer).start()
        wait_w(1, layer)

        @pl.when(first)
        def _():
            load_w(3, 0)
        rs_run(0, lambda c: mm(attn[layer], wo[:, chunk(c)]))

        @pl.when(first)
        def _():
            load_w(1, 1)
        res[...] = res[...] + own[...] + bias_ref[layer, 0:1]

        h2_g[layer, me] = normed(res[...], lnp[2:3], lnp[3:4], xh2, rs2, layer)
        ag_start(h2_g, layer)
        acc[...] = jnp.zeros_like(acc)
        wait_w(2, layer)

        def up_chunk(c):
            h = h2_g[layer, :, :, chunk(c)].reshape(SEQ, C)
            for n in range(0, FF, C):
                acc[:, n:n + C] += mm(h, wu[chunk(c), n:n + C])
        ag_consume(h2_g, layer, up_chunk)
        out_copy(1, h2_g, h2_o, layer).start()

        @pl.when(first)
        def _():
            load_w(2, 1)

        @pl.loop(0, FF // C)
        def _(c):
            pre = acc[:, chunk(c)] + bup_ref[pl.ds(layer, 1), chunk(c)]
            sq = pre * pre
            t = jnp.tanh(GELU_K * (pre + GELU_C * (sq * pre)))
            cdf = 0.5 * (1.0 + t)
            act[layer, :, chunk(c)] = (pre * cdf).astype(BF16)
            gp[layer, :, chunk(c)] = cdf + 0.5 * pre * (1.0 - t * t) * (GELU_K * (1.0 + 3.0 * GELU_C * sq))
        out_copy(5, act, act_o, layer).start()
        wait_w(3, layer)
        rs_run(1, lambda c: mm(act[layer], wd[:, chunk(c)]))

        @pl.when(first)
        def _():
            load_w(3, 1)
        res[...] = res[...] + own[...] + bias_ref[layer, 1:2]

    y_ref[...] = res[...].astype(BF16)
    res[...] = dy_ref[0].astype(F32)
    sg[...] = jnp.zeros_like(sg)

    @pl.loop(0, N_LAYERS)
    def _(step):
        layer = N_LAYERS - 1 - step
        top = step == 0
        low = step == N_LAYERS - 1
        lnp = ln_ref[layer]
        sg[layer, 5:6, :] = jnp.sum(res[...], axis=0, keepdims=True)
        dm_g[layer, me] = res[...].astype(BF16)
        ag_start(dm_g, layer)
        acct[...] = jnp.zeros_like(acct)

        @pl.when(low)
        def _():
            wait_w(3, 0)

        def dact_chunk(c):
            g = dm_g[layer, :, :, chunk(c)].reshape(SEQ, C)
            for n in range(0, FF, C):
                acct[n:n + C, :] += mm_nt(wd[n:n + C, chunk(c)], g)
        ag_consume(dm_g, layer, dact_chunk)
        out_copy(2, dm_g, dm_o, layer).start()

        @pl.when(top)
        def _():
            load_w(3, 0)

        @pl.loop(0, FF // C)
        def _(c):
            d_pre = acct[chunk(c), :].T * gp[layer, :, chunk(c)]
            bupg_ref[pl.ds(layer, 1), chunk(c)] = jnp.sum(d_pre, axis=0, keepdims=True)
            dpre[layer, :, chunk(c)] = d_pre.astype(BF16)
        out_copy(6, dpre, dpre_o, layer).start()

        @pl.when(low)
        def _():
            wait_w(2, 0)
        rs_run(0, lambda c: mm_nt(wu[chunk(c), :], dpre[layer]).T)

        @pl.when(top)
        def _():
            load_w(2, 0)
        res[...] = res[...] + norm_grad(own[...], lnp[2:3], xh2, rs2, layer, 2)

        sg[layer, 4:5, :] = jnp.sum(res[...], axis=0, keepdims=True)
        da_g[layer, me] = res[...].astype(BF16)
        ag_start(da_g, layer)
        acct[0:ATT, :] = jnp.zeros((ATT, SEQ), F32)

        @pl.when(low)
        def _():
            wait_w(1, 0)

        def dattn_chunk(c):
            g = da_g[layer, :, :, chunk(c)].reshape(SEQ, C)
            acct[0:ATT, :] += mm_nt(wo[:, chunk(c)], g)
        ag_consume(da_g, layer, dattn_chunk)
        out_copy(3, da_g, da_o, layer).start()

        @pl.when(top)
        def _():
            load_w(1, 0)

        @pl.when(low)
        def _():
            for copy in small_copies(N_LAYERS - 1):
                copy.start()

        for hd in range(HEADS):
            q = qkv[layer, :, hd * HD:(hd + 1) * HD]
            k = qkv[layer, :, ATT + hd * HD:ATT + (hd + 1) * HD]
            v = qkv[layer, :, 2 * ATT + hd * HD:2 * ATT + (hd + 1) * HD]
            p = prob[layer, hd]
            d_o = acct[hd * HD:(hd + 1) * HD, :].T.astype(BF16)
            d_p = mm_nt(d_o, v)
            d_v = mm(p.T, d_o)
            pf = p.astype(F32)
            dot = jnp.sum(d_p * pf, axis=-1, keepdims=True)
            d_s = (pf * (d_p - dot) * SCALE).astype(BF16)
            dqkv[layer, :, hd * HD:(hd + 1) * HD] = mm(d_s, k).astype(BF16)
            dqkv[layer, :, ATT + hd * HD:ATT + (hd + 1) * HD] = mm(d_s.T, q).astype(BF16)
            dqkv[layer, :, 2 * ATT + hd * HD:2 * ATT + (hd + 1) * HD] = d_v.astype(BF16)
        out_copy(7, dqkv, dqkv_o, layer).start()

        @pl.when(low)
        def _():
            wait_w(0, 0)
        rs_run(1, lambda c: mm_nt(wq[chunk(c), :], dqkv[layer]).T)

        @pl.when(top)
        def _():
            load_w(0, 0)
        res[...] = res[...] + norm_grad(own[...], lnp[0:1], xh1, rs1, layer, 0)

    for copy in small_copies(0):
        copy.start()
    xg_ref[...] = res[...].astype(BF16)
    for layer in reversed(range(N_LAYERS)):
        for copy in small_copies(layer):
            copy.wait()
        small_ref[layer] = (sg[layer] + sgr[layer, 0]) + (sgr[layer, 1] + sgr[layer, 2])
    for layer in range(N_LAYERS):
        for i, (src, dst) in enumerate(outs):
            out_copy(i, src, dst, layer).wait()


def grads_kernel(y_in, xg_in, small_in, bupg_in, h_h, h2_h, dm_h, da_h, a_h, act_h, dpre_h, dqkv_h,
                 y_o, xg_o, lng_o, biasg_o, wqkv_o, wo_o, wu_o, bupg_o, wd_o,
                 h, h2, dm, da, attn, act, dpre, dqkv, big, qbuf, obuf, isem, bsem, qsem, osem):
    ins = [(dm_h, dm), (act_h, act), (h2_h, h2), (dpre_h, dpre), (da_h, da), (a_h, attn), (h_h, h), (dqkv_h, dqkv)]

    def in_copy(i, layer):
        return pltpu.make_async_copy(ins[i][0].at[layer], ins[i][1].at[layer], isem.at[i, layer])

    for layer in reversed(range(N_LAYERS)):
        for i in range(len(ins)):
            in_copy(i, layer).start()
    y_o[...] = y_in[...]
    xg_o[...] = xg_in[...]
    lng_o[...] = small_in[:, 0:4, :]
    biasg_o[...] = small_in[:, 4:6, :]
    bupg_o[...] = bupg_in[...]

    def big_copy(dst, layer, c, slot):
        return pltpu.make_async_copy(big.at[slot], dst.at[layer, chunk(c)], bsem.at[slot])

    def q_copy(layer, c, slot):
        return pltpu.make_async_copy(qbuf.at[slot], wqkv_o.at[layer, :, chunk(c), :], qsem.at[slot])

    def o_copy(layer, c):
        return pltpu.make_async_copy(obuf.at[c], wo_o.at[layer, pl.ds(c * (ATT // 2), ATT // 2)], osem.at[c])

    for step, layer in enumerate(reversed(range(N_LAYERS))):
        for w, (dst, left, right) in enumerate(((wd_o, act, dm), (wu_o, h2, dpre))):
            in_copy(2 * w, layer).wait()
            in_copy(2 * w + 1, layer).wait()
            base = (2 * step + w) * NC

            @pl.loop(0, NC)
            def _(c):
                slot = lax.rem(base + c, 3)

                @pl.when(base + c >= 3)
                def _():
                    big_copy(dst, layer, c, slot).wait()
                lt = left[layer, :, chunk(c)].T
                for n in range(0, D, C):
                    big[slot, :, n:n + C] = mm(lt, right[layer, :, n:n + C]).astype(BF16)
                big_copy(dst, layer, c, slot).start()
        in_copy(4, layer).wait()
        in_copy(5, layer).wait()
        for c in range(2):
            if step > 0:
                o_copy(layer, c).wait()
            lt = attn[layer, :, :].T[c * (ATT // 2):(c + 1) * (ATT // 2)]
            for n in range(0, D, C):
                obuf[c, :, n:n + C] = mm(lt, da[layer, :, n:n + C]).astype(BF16)
            o_copy(layer, c).start()
        in_copy(6, layer).wait()
        in_copy(7, layer).wait()
        qbase = step * NC

        @pl.loop(0, NC)
        def _(c):
            slot = lax.rem(qbase + c, 3)

            @pl.when(qbase + c >= 3)
            def _():
                q_copy(layer, c, slot).wait()
            lt = h[layer, :, chunk(c)].T
            for n in range(0, QKV, 3 * HD):
                vals = mm(lt, dqkv[layer, :, n:n + 3 * HD]).astype(BF16)
                for j in range(3):
                    qbuf[slot, n // HD + j] = vals[:, j * HD:(j + 1) * HD]
            q_copy(layer, c, slot).start()
    for slot in range(3):
        big_copy(wu_o, 0, 0, slot).wait()
        q_copy(0, 0, slot).wait()
    for c in range(2):
        o_copy(0, c).wait()


def solution(mesh):
    vmem = pl.BlockSpec(memory_space=pltpu.VMEM)
    hbm = pl.BlockSpec(memory_space=pl.ANY)

    def device_step(x_loc, dy_loc, ln_par, bias_d, w_qkv, w_out, w_up, b_up, w_down):
        wqkv_t = jnp.transpose(w_qkv, (0, 2, 3, 1, 4)).reshape(N_LAYERS, 3 * HEADS, D, HD)
        wo_t = w_out.reshape(N_LAYERS, ATT, D)
        sds = jax.ShapeDtypeStruct
        gath = (N_LAYERS, 4, BLK, D)
        dma = pltpu.SemaphoreType.DMA
        chain_out = pl.pallas_call(
            chain_kernel,
            name='chain',
            out_shape=(sds((BLK, D), BF16), sds((BLK, D), BF16), sds((N_LAYERS, 8, D), F32), sds((N_LAYERS, FF), F32),
                       sds(gath, BF16), sds(gath, BF16), sds(gath, BF16), sds(gath, BF16),
                       sds((N_LAYERS, SEQ, ATT), BF16), sds((N_LAYERS, SEQ, FF), BF16), sds((N_LAYERS, SEQ, FF), BF16),
                       sds((N_LAYERS, SEQ, QKV), BF16)),
            in_specs=[vmem] * 5 + [hbm] * 4,
            out_specs=tuple([vmem] * 4 + [hbm] * 8),
            scratch_shapes=[
                pltpu.VMEM((D, QKV), BF16), pltpu.VMEM((ATT, D), BF16), pltpu.VMEM((D, FF), BF16), pltpu.VMEM((FF, D), BF16),
                pltpu.VMEM(gath, BF16), pltpu.VMEM(gath, BF16), pltpu.VMEM(gath, BF16), pltpu.VMEM(gath, BF16),
                pltpu.VMEM((N_LAYERS, SEQ, QKV), BF16), pltpu.VMEM((N_LAYERS, HEADS, SEQ, SEQ), BF16),
                pltpu.VMEM((N_LAYERS, SEQ, ATT), BF16), pltpu.VMEM((N_LAYERS, SEQ, FF), BF16), pltpu.VMEM((N_LAYERS, SEQ, FF), F32),
                pltpu.VMEM((N_LAYERS, SEQ, FF), BF16), pltpu.VMEM((N_LAYERS, SEQ, QKV), BF16),
                pltpu.VMEM((N_LAYERS, BLK, D), F32), pltpu.VMEM((N_LAYERS, BLK, D), F32),
                pltpu.VMEM((N_LAYERS, BLK, 128), F32), pltpu.VMEM((N_LAYERS, BLK, 128), F32),
                pltpu.VMEM((BLK, D), F32), pltpu.VMEM((SEQ, D), F32), pltpu.VMEM((D, SEQ), F32),
                pltpu.VMEM((2, 2, BLK, D), F32), pltpu.VMEM((BLK, D), F32), pltpu.VMEM((2, 2, BLK, D), F32),
                pltpu.VMEM((2, BLK, D), BF16), pltpu.VMEM((BLK, D), BF16),
                pltpu.VMEM((N_LAYERS, 8, D), F32), pltpu.VMEM((N_LAYERS, 3, 8, D), F32),
                dma((4, 3 * HEADS)), dma((8, N_LAYERS)), dma((6, NC)), dma((2, 4, NC)), dma((N_LAYERS, 2, 3)),
            ],
            compiler_params=pltpu.CompilerParams(collective_id=0, has_side_effects=True, vmem_limit_bytes=VMEM_ALL),
        )(x_loc, dy_loc, ln_par, bias_d, b_up, wqkv_t, wo_t, w_up, w_down)
        y_loc, xg_loc, small, bupg, h, h2, dm, da, attn, act, dpre, dqkv = chain_out
        flat = (N_LAYERS, SEQ, D)
        y_out, x_grad, lng, biasg, wqkv_g, wo_g, wu_g, bupg_o, wd_g = pl.pallas_call(
            grads_kernel,
            name='grads',
            out_shape=(sds((BLK, D), BF16), sds((BLK, D), BF16), sds((N_LAYERS, 4, D), F32), sds((N_LAYERS, 2, D), F32),
                       sds((N_LAYERS, 3 * HEADS, D, HD), BF16), sds((N_LAYERS, ATT, D), BF16), sds((N_LAYERS, D, FF), BF16),
                       sds((N_LAYERS, FF), F32), sds((N_LAYERS, FF, D), BF16)),
            in_specs=[vmem] * 4 + [hbm] * 8,
            out_specs=(vmem, vmem, vmem, vmem, hbm, hbm, hbm, vmem, hbm),
            scratch_shapes=[
                pltpu.VMEM(flat, BF16), pltpu.VMEM(flat, BF16), pltpu.VMEM(flat, BF16), pltpu.VMEM(flat, BF16),
                pltpu.VMEM((N_LAYERS, SEQ, ATT), BF16), pltpu.VMEM((N_LAYERS, SEQ, FF), BF16), pltpu.VMEM((N_LAYERS, SEQ, FF), BF16),
                pltpu.VMEM((N_LAYERS, SEQ, QKV), BF16),
                pltpu.VMEM((3, C, D), BF16), pltpu.VMEM((3, 3 * HEADS, C, HD), BF16), pltpu.VMEM((2, ATT // 2, D), BF16),
                dma((8, N_LAYERS)), dma((3,)), dma((3,)), dma((2,)),
            ],
            compiler_params=pltpu.CompilerParams(vmem_limit_bytes=VMEM_ALL),
        )(y_loc, xg_loc, small, bupg, h.reshape(flat), h2.reshape(flat), dm.reshape(flat), da.reshape(flat), attn, act, dpre, dqkv)
        wqkv_g = jnp.transpose(wqkv_g.reshape(N_LAYERS, 3, HEADS, D, HD), (0, 3, 1, 2, 4))
        return (y_out[None], x_grad[None], lng, biasg, wqkv_g, wo_g.reshape(N_LAYERS, HEADS, HD, D), wu_g, bupg_o, wd_g)

    in_specs = (P('dp', 'tp', None), P('dp', 'tp', None), P(None, None, None), P(None, None, None),
                P(None, None, None, 'tp', None), P(None, 'tp', None, None), P(None, None, 'tp'), P(None, 'tp'), P(None, 'tp', None))
    out_specs = (P('dp', 'tp', None), P('dp', 'tp', None), P('dp', None, None), P('dp', None, None),
                 P('dp', None, None, 'tp', None), P('dp', 'tp', None, None), P('dp', None, 'tp'), P('dp', 'tp'), P('dp', 'tp', None))
    return jax.shard_map(device_step, mesh=mesh, in_specs=in_specs, out_specs=out_specs, check_vma=False)
```

profile of v0, /device:TPU:0, one launch (start us, length us, event | category | flops | bytes accessed | tf_op | source)
XLA Modules:
  0.0 179.0 jit_solution(596117230071360382)
XLA Ops:
  0.6 147.0 %chain.1 = (bf16[32,2560]{1,0:T(8,128)(2,1)}, bf16[32,2560]{1,0:T(8,128)(2,1)}, f32[2,8,2560]{2,1,0:T(8,128)}, f32[2,2560]{1,0:T(2,128)}, bf16[2,4,32,2560]{3,2,...) custom-call(bf16[1,32,2560]{2,1,0:T(8,128)(2,1)} %x_ref.1, ...), custom_call_target="tpu_custom_call" | custom-call | tf_op jit(solution)/shard_map/chain/pallas_call | solution.py:456
  147.7 31.3 %grads.1 = (bf16[32,2560]{1,0:T(8,128)(2,1)}, bf16[32,2560]{1,0:T(8,128)(2,1)}, f32[2,4,2560]{2,1,0:T(4,128)}, f32[2,2,2560]{2,1,0:T(2,128)}, bf16[2,15,2560,128...) custom-call(bf16[32,2560]{1,0:T(8,128)(2,1)} %get-tuple-element.30.y, ...), custom_call_target="tpu_custom_call" | custom-call | tf_op jit(solution)/shard_map/grads/pallas_call | solution.py:483
where the time goes:
time: 179 us
  Pallas kernels  178 us (99%)
    pallas_call x1, Pallas kernels, device_step(): pl.pallas_call(chain_kernel, name='chain', out_shape=(sds((BLK, D), BF16)...  147 us
    pallas_call x1, Pallas kernels, device_step(): pl.pallas_call(grads_kernel, name='grads', out_shape=(sds((BLK, D), BF16)...  31.3 us

commit v1 on v0

--- a/solution.py
+++ b/solution.py
@@ -37,7 +37,7 @@
 def chain_kernel(x_ref, dy_ref, ln_ref, bias_ref, bup_ref, wqkv_h, wo_h, wu_h, wd_h,
                  y_ref, xg_ref, small_ref, bupg_ref, h_o, h2_o, dm_o, da_o, a_o, act_o, dpre_o, dqkv_o,
                  wq, wo, wu, wd, h_g, h2_g, dm_g, da_g, qkv, prob, attn, act, gp, dpre, dqkv,
-                 xh1, xh2, rs1, rs2, res, acc, acct, part, own, rr, xx, ss, sg, sgr,
+                 xh1, xh2, rs1, rs2, res, dres, acc, acct, part, own, rr, xx, ss, sg, sgr,
                  wsem, osem, agsem, rssem, gsem):
     me = lax.axis_index('tp')
     x_id = lax.div(me, 2)
@@ -71,23 +71,36 @@
 
     outs = [(h_g, h_o), (h2_g, h2_o), (dm_g, dm_o), (da_g, da_o), (attn, a_o), (act, act_o), (dpre, dpre_o), (dqkv, dqkv_o)]
 
-    def ag_side(g, layer, c):
+    def ag_side(g, layer, c, k=0):
         mine = g.at[layer, me, :, chunk(c)]
-        return remote(mine, mine, agsem.at[0, c], agsem.at[1, c], sib)
-
-    def ag_across(g, layer, c):
+        return remote(mine, mine, agsem.at[k, 0, c], agsem.at[k, 1, c], sib)
+
+    def ag_across(g, layer, c, k=0):
         mine = g.at[layer, me, :, chunk(c)]
-        return remote(mine, mine, agsem.at[2, c], agsem.at[3, c], cross)
-
-    def ag_forward(g, layer, c):
+        return remote(mine, mine, agsem.at[k, 2, c], agsem.at[k, 3, c], cross)
+
+    def ag_forward(g, layer, c, k=0):
         theirs = g.at[layer, cross, :, chunk(c)]
-        return remote(theirs, theirs, agsem.at[4, c], agsem.at[5, c], sib)
-
-    def ag_start(g, layer):
+        return remote(theirs, theirs, agsem.at[k, 4, c], agsem.at[k, 5, c], sib)
+
+    def ag_relay(g, layer, k):
+        @pl.loop(0, NC)
+        def _(c):
+            ag_across(g, layer, c, k).wait_recv()
+            ag_forward(g, layer, c, k).start()
+
+    def ag_finish(g, layer, k):
+        @pl.loop(0, NC)
+        def _(c):
+            ag_side(g, layer, c, k).wait()
+            ag_forward(g, layer, c, k).wait()
+            ag_across(g, layer, c, k).wait_send()
+
+    def ag_start(g, layer, k=0):
         for c in range(NC):
-            ag_across(g, layer, c).start()
+            ag_across(g, layer, c, k).start()
         for c in range(NC):
-            ag_side(g, layer, c).start()
+            ag_side(g, layer, c, k).start()
 
     def ag_consume(g, layer, compute):
         @pl.loop(0, NC + 1)
@@ -111,19 +124,22 @@
             ag_forward(g, layer, c).wait_send()
 
     def rs_side(par, c):
-        return remote(part.at[:, 1 - core, :, chunk(c)], rr.at[par, :, :, chunk(c)], rssem.at[par, 0, c], rssem.at[par, 1, c], sib)
+        return remote(part.at[par // 2, :, 1 - core, :, chunk(c)], rr.at[par, :, :, chunk(c)],
+                      rssem.at[par, 0, c], rssem.at[par, 1, c], sib)
 
     def rs_across(par, c):
-        return remote(ss.at[:, chunk(c)], xx.at[par, :, chunk(c)], rssem.at[par, 2, c], rssem.at[par, 3, c], cross)
-
-    def rs_run(par, compute, lag=2):
+        return remote(ss.at[par // 2, :, chunk(c)], xx.at[par, :, chunk(c)], rssem.at[par, 2, c], rssem.at[par, 3, c], cross)
+
+    def rs_send(par, compute, lag=2):
+        buf = par // 2
+
         @pl.loop(0, NC + lag)
         def _(c):
             @pl.when(c < NC)
             def _():
                 vals = compute(c)
                 for b in range(4):
-                    part[b // 2, b % 2, :, chunk(c)] = vals[b * BLK:(b + 1) * BLK]
+                    part[buf, b // 2, b % 2, :, chunk(c)] = vals[b * BLK:(b + 1) * BLK]
                 rs_side(par, c).start()
 
             @pl.when(c >= lag)
@@ -131,16 +147,17 @@
                 cc = c - lag
                 rs_side(par, cc).wait_recv()
                 cols = chunk(cc)
-                ss[:, cols] = (part[1 - x_id, core, :, cols] + rr[par, 1 - x_id, :, cols]).astype(BF16)
+                ss[buf, :, cols] = (part[buf, 1 - x_id, core, :, cols] + rr[par, 1 - x_id, :, cols]).astype(BF16)
                 rs_across(par, cc).start()
-                own[:, cols] = part[x_id, core, :, cols] + rr[par, x_id, :, cols]
-
+                own[buf, :, cols] = part[buf, x_id, core, :, cols] + rr[par, x_id, :, cols]
+
+    def rs_finish(par):
         @pl.loop(0, NC)
         def _(c):
             rs_across(par, c).wait_recv()
             rs_side(par, c).wait_send()
             rs_across(par, c).wait_send()
-            own[:, chunk(c)] += xx[par, :, chunk(c)].astype(F32)
+            own[par // 2, :, chunk(c)] += xx[par, :, chunk(c)].astype(F32)
 
     def normed(vals, gain, shift, xh, rs, layer):
         mean_val = jnp.mean(vals, axis=-1, keepdims=True)
@@ -176,9 +193,21 @@
     col_id = lax.broadcasted_iota(jnp.int32, (SEQ, SEQ), 1)
     causal = row_id >= col_id
 
+    def dact_chunk(c):
+        g = dm_g[0, :, :, chunk(c)].reshape(SEQ, C)
+        acct[...] += mm_nt(wd[:, chunk(c)], g)
+
+    def dact_early(layer, lo, hi):
+        @pl.when(layer == N_LAYERS - 1)
+        def _():
+            @pl.loop(lo, hi)
+            def _(c):
+                acct[chunk(c), :] = mm_nt(wd[chunk(c), :], dm_g[N_LAYERS - 1].reshape(SEQ, D))
+
     @pl.loop(0, N_LAYERS)
     def _(layer):
         first = layer == 0
+        last = layer == N_LAYERS - 1
         lnp = ln_ref[layer]
         h_g[layer, me] = normed(res[...], lnp[0:1], lnp[1:2], xh1, rs1, layer)
         ag_start(h_g, layer)
@@ -200,6 +229,8 @@
         @pl.when(first)
         def _():
             load_w(0, 1)
+            dm_g[N_LAYERS - 1, me] = dy_ref[0]
+            ag_start(dm_g, N_LAYERS - 1, 1)
 
         for j in range(3 * HEADS):
             qkv[layer, :, j * HD:(j + 1) * HD] = acc[:, j * HD:(j + 1) * HD].astype(BF16)
@@ -218,17 +249,29 @@
         @pl.when(first)
         def _():
             load_w(3, 0)
-        rs_run(0, lambda c: mm(attn[layer], wo[:, chunk(c)]))
+        @pl.when(first)
+        def _():
+            ag_relay(dm_g, N_LAYERS - 1, 1)
+
+        @pl.when(last)
+        def _():
+            wait_w(3, N_LAYERS - 1)
+        rs_send(0, lambda c: mm(attn[layer], wo[:, chunk(c)]))
+        dact_early(layer, 0, 2)
+        rs_finish(0)
 
         @pl.when(first)
         def _():
             load_w(1, 1)
-        res[...] = res[...] + own[...] + bias_ref[layer, 0:1]
+            ag_finish(dm_g, N_LAYERS - 1, 1)
+            out_copy(2, dm_g, dm_o, N_LAYERS - 1).start()
+        res[...] = res[...] + own[0] + bias_ref[layer, 0:1]
 
         h2_g[layer, me] = normed(res[...], lnp[2:3], lnp[3:4], xh2, rs2, layer)
         ag_start(h2_g, layer)
         acc[...] = jnp.zeros_like(acc)
         wait_w(2, layer)
+        dact_early(layer, 2, NC)
 
         def up_chunk(c):
             h = h2_g[layer, :, :, chunk(c)].reshape(SEQ, C)
@@ -250,16 +293,16 @@
             act[layer, :, chunk(c)] = (pre * cdf).astype(BF16)
             gp[layer, :, chunk(c)] = cdf + 0.5 * pre * (1.0 - t * t) * (GELU_K * (1.0 + 3.0 * GELU_C * sq))
         out_copy(5, act, act_o, layer).start()
-        wait_w(3, layer)
-        rs_run(1, lambda c: mm(act[layer], wd[:, chunk(c)]))
-
-        @pl.when(first)
-        def _():
+
+        @pl.when(first)
+        def _():
+            wait_w(3, 0)
+            rs_send(1, lambda c: mm(act[0], wd[:, chunk(c)]))
+            rs_finish(1)
             load_w(3, 1)
-        res[...] = res[...] + own[...] + bias_ref[layer, 1:2]
-
-    y_ref[...] = res[...].astype(BF16)
-    res[...] = dy_ref[0].astype(F32)
+            res[...] = res[...] + own[0] + bias_ref[0, 1:2]
+
+    dres[...] = dy_ref[0].astype(F32)
     sg[...] = jnp.zeros_like(sg)
 
     @pl.loop(0, N_LAYERS)
@@ -268,25 +311,15 @@
         top = step == 0
         low = step == N_LAYERS - 1
         lnp = ln_ref[layer]
-        sg[layer, 5:6, :] = jnp.sum(res[...], axis=0, keepdims=True)
-        dm_g[layer, me] = res[...].astype(BF16)
-        ag_start(dm_g, layer)
-        acct[...] = jnp.zeros_like(acct)
-
+        sg[layer, 5:6, :] = jnp.sum(dres[...], axis=0, keepdims=True)
         @pl.when(low)
         def _():
+            dm_g[0, me] = dres[...].astype(BF16)
+            ag_start(dm_g, 0)
+            acct[...] = jnp.zeros_like(acct)
             wait_w(3, 0)
-
-        def dact_chunk(c):
-            g = dm_g[layer, :, :, chunk(c)].reshape(SEQ, C)
-            for n in range(0, FF, C):
-                acct[n:n + C, :] += mm_nt(wd[n:n + C, chunk(c)], g)
-        ag_consume(dm_g, layer, dact_chunk)
-        out_copy(2, dm_g, dm_o, layer).start()
-
-        @pl.when(top)
-        def _():
-            load_w(3, 0)
+            ag_consume(dm_g, 0, dact_chunk)
+            out_copy(2, dm_g, dm_o, 0).start()
 
         @pl.loop(0, FF // C)
         def _(c):
@@ -298,15 +331,18 @@
         @pl.when(low)
         def _():
             wait_w(2, 0)
-        rs_run(0, lambda c: mm_nt(wu[chunk(c), :], dpre[layer]).T)
+        rs_send(0, lambda c: mm_nt(wu[chunk(c), :], dpre[layer]).T)
 
         @pl.when(top)
         def _():
             load_w(2, 0)
-        res[...] = res[...] + norm_grad(own[...], lnp[2:3], xh2, rs2, layer, 2)
-
-        sg[layer, 4:5, :] = jnp.sum(res[...], axis=0, keepdims=True)
-        da_g[layer, me] = res[...].astype(BF16)
+            rs_send(2, lambda c: mm(act[N_LAYERS - 1], wd[:, chunk(c)]))
+            load_w(3, 0)
+        rs_finish(0)
+        dres[...] = dres[...] + norm_grad(own[0], lnp[2:3], xh2, rs2, layer, 2)
+
+        sg[layer, 4:5, :] = jnp.sum(dres[...], axis=0, keepdims=True)
+        da_g[layer, me] = dres[...].astype(BF16)
         ag_start(da_g, layer)
         acct[0:ATT, :] = jnp.zeros((ATT, SEQ), F32)
 
@@ -323,6 +359,8 @@
         @pl.when(top)
         def _():
             load_w(1, 0)
+            rs_finish(2)
+            y_ref[...] = (res[...] + own[1] + bias_ref[N_LAYERS - 1, 1:2]).astype(BF16)
 
         @pl.when(low)
         def _():
@@ -348,16 +386,17 @@
         @pl.when(low)
         def _():
             wait_w(0, 0)
-        rs_run(1, lambda c: mm_nt(wq[chunk(c), :], dqkv[layer]).T)
+        rs_send(1, lambda c: mm_nt(wq[chunk(c), :], dqkv[layer]).T)
+        rs_finish(1)
 
         @pl.when(top)
         def _():
             load_w(0, 0)
-        res[...] = res[...] + norm_grad(own[...], lnp[0:1], xh1, rs1, layer, 0)
+        dres[...] = dres[...] + norm_grad(own[0], lnp[0:1], xh1, rs1, layer, 0)
 
     for copy in small_copies(0):
         copy.start()
-    xg_ref[...] = res[...].astype(BF16)
+    xg_ref[...] = dres[...].astype(BF16)
     for layer in reversed(range(N_LAYERS)):
         for copy in small_copies(layer):
             copy.wait()
@@ -375,9 +414,15 @@
     def in_copy(i, layer):
         return pltpu.make_async_copy(ins[i][0].at[layer], ins[i][1].at[layer], isem.at[i, layer])
 
-    for layer in reversed(range(N_LAYERS)):
-        for i in range(len(ins)):
-            in_copy(i, layer).start()
+    order = [(i, layer) for layer in reversed(range(N_LAYERS)) for i in range(0, len(ins), 2)]
+
+    def prefetch(k):
+        if k < len(order):
+            in_copy(order[k][0], order[k][1]).start()
+            in_copy(order[k][0] + 1, order[k][1]).start()
+
+    prefetch(0)
+    prefetch(1)
     y_o[...] = y_in[...]
     xg_o[...] = xg_in[...]
     lng_o[...] = small_in[:, 0:4, :]
@@ -397,6 +442,7 @@
         for w, (dst, left, right) in enumerate(((wd_o, act, dm), (wu_o, h2, dpre))):
             in_copy(2 * w, layer).wait()
             in_copy(2 * w + 1, layer).wait()
+            prefetch(4 * step + w + 2)
             base = (2 * step + w) * NC
 
             @pl.loop(0, NC)
@@ -412,6 +458,7 @@
                 big_copy(dst, layer, c, slot).start()
         in_copy(4, layer).wait()
         in_copy(5, layer).wait()
+        prefetch(4 * step + 4)
         for c in range(2):
             if step > 0:
                 o_copy(layer, c).wait()
@@ -421,6 +468,7 @@
             o_copy(layer, c).start()
         in_copy(6, layer).wait()
         in_copy(7, layer).wait()
+        prefetch(4 * step + 5)
         qbase = step * NC
 
         @pl.loop(0, NC)
@@ -470,11 +518,11 @@
                 pltpu.VMEM((N_LAYERS, SEQ, FF), BF16), pltpu.VMEM((N_LAYERS, SEQ, QKV), BF16),
                 pltpu.VMEM((N_LAYERS, BLK, D), F32), pltpu.VMEM((N_LAYERS, BLK, D), F32),
                 pltpu.VMEM((N_LAYERS, BLK, 128), F32), pltpu.VMEM((N_LAYERS, BLK, 128), F32),
-                pltpu.VMEM((BLK, D), F32), pltpu.VMEM((SEQ, D), F32), pltpu.VMEM((D, SEQ), F32),
-                pltpu.VMEM((2, 2, BLK, D), F32), pltpu.VMEM((BLK, D), F32), pltpu.VMEM((2, 2, BLK, D), F32),
-                pltpu.VMEM((2, BLK, D), BF16), pltpu.VMEM((BLK, D), BF16),
+                pltpu.VMEM((BLK, D), F32), pltpu.VMEM((BLK, D), F32), pltpu.VMEM((SEQ, D), F32), pltpu.VMEM((D, SEQ), F32),
+                pltpu.VMEM((2, 2, 2, BLK, D), F32), pltpu.VMEM((2, BLK, D), F32), pltpu.VMEM((3, 2, BLK, D), F32),
+                pltpu.VMEM((3, BLK, D), BF16), pltpu.VMEM((2, BLK, D), BF16),
                 pltpu.VMEM((N_LAYERS, 8, D), F32), pltpu.VMEM((N_LAYERS, 3, 8, D), F32),
-                dma((4, 3 * HEADS)), dma((8, N_LAYERS)), dma((6, NC)), dma((2, 4, NC)), dma((N_LAYERS, 2, 3)),
+                dma((4, 3 * HEADS)), dma((8, N_LAYERS)), dma((2, 6, NC)), dma((3, 4, NC)), dma((N_LAYERS, 2, 3)),
             ],
             compiler_params=pltpu.CompilerParams(collective_id=0, has_side_effects=True, vmem_limit_bytes=VMEM_ALL),
         )(x_loc, dy_loc, ln_par, bias_d, b_up, wqkv_t, wo_t, w_up, w_down)

time: 179 us -> 169 us (0.944)
  Pallas kernels: 178 us -> 168 us
    pallas_call x1, Pallas kernels: 147 us -> 137 us  [device_step(): pl.pallas_call(chain_kernel, name='chain', out_shape=(sds((BLK, D), BF16)...]
where the time goes in v1:
time: 169 us
  Pallas kernels  168 us (99%)
    pallas_call x1, Pallas kernels, device_step(): pl.pallas_call(chain_kernel, name='chain', out_shape=(sds((BLK, D), BF16)...  137 us
    pallas_call x1, Pallas kernels, device_step(): pl.pallas_call(grads_kernel, name='grads', out_shape=(sds((BLK, D), BF16)...  31.5 us

profile of v1, /device:TPU:0, one launch (start us, length us, event | category | flops | bytes accessed | tf_op | source)
XLA Modules:
  0.0 169.1 jit_solution(1206697533477670579)
XLA Ops:
  0.6 136.9 %chain.1 = (bf16[32,2560]{1,0:T(8,128)(2,1)}, bf16[32,2560]{1,0:T(8,128)(2,1)}, f32[2,8,2560]{2,1,0:T(8,128)}, f32[2,2560]{1,0:T(2,128)}, bf16[2,4,32,2560]{3,2,...) custom-call(bf16[1,32,2560]{2,1,0:T(8,128)(2,1)} %x_ref.1, ...), custom_call_target="tpu_custom_call" | custom-call | tf_op jit(solution)/shard_map/chain/pallas_call | solution.py:504
  137.6 31.5 %grads.1 = (bf16[32,2560]{1,0:T(8,128)(2,1)}, bf16[32,2560]{1,0:T(8,128)(2,1)}, f32[2,4,2560]{2,1,0:T(4,128)}, f32[2,2,2560]{2,1,0:T(2,128)}, bf16[2,15,2560,128...) custom-call(bf16[32,2560]{1,0:T(8,128)(2,1)} %get-tuple-element.30.y, ...), custom_call_target="tpu_custom_call" | custom-call | tf_op jit(solution)/shard_map/grads/pallas_call | solution.py:531

commit v2 on v1

--- a/solution.py
+++ b/solution.py
@@ -12,6 +12,7 @@
 QKV = 3 * ATT
 C = 512
 NC = D // C
+SLOTS = 4
 SCALE = HD ** -0.5
 GELU_K = 0.7978845608028654
 GELU_C = 0.044715
@@ -35,9 +36,9 @@
 
 
 def chain_kernel(x_ref, dy_ref, ln_ref, bias_ref, bup_ref, wqkv_h, wo_h, wu_h, wd_h,
-                 y_ref, xg_ref, small_ref, bupg_ref, h_o, h2_o, dm_o, da_o, a_o, act_o, dpre_o, dqkv_o,
+                 y_ref, xg_ref, small1_ref, small2_ref, bupg_ref, h_o, h2_o, dm_o, da_o, a_o, act_o, dpre_o, dqkv_o,
                  wq, wo, wu, wd, h_g, h2_g, dm_g, da_g, qkv, prob, attn, act, gp, dpre, dqkv,
-                 xh1, xh2, rs1, rs2, res, dres, acc, acct, part, own, rr, xx, ss, sg, sgr,
+                 xh1, xh2, rs1, rs2, res, dres, acc, acct, part, own, rr, xx, ss, sg1, sg2, sgr1, sgr2,
                  wsem, osem, agsem, rssem, gsem):
     me = lax.axis_index('tp')
     x_id = lax.div(me, 2)
@@ -102,17 +103,17 @@
         for c in range(NC):
             ag_side(g, layer, c, k).start()
 
-    def ag_consume(g, layer, compute):
-        @pl.loop(0, NC + 1)
+    def ag_consume(g, layer, compute, lag=2):
+        @pl.loop(0, NC + lag)
         def _(c):
             @pl.when(c < NC)
             def _():
                 ag_across(g, layer, c).wait_recv()
                 ag_forward(g, layer, c).start()
 
-            @pl.when(c >= 1)
+            @pl.when(c >= lag)
             def _():
-                cc = c - 1
+                cc = c - lag
                 ag_side(g, layer, cc).wait_recv()
                 ag_forward(g, layer, cc).wait_recv()
                 compute(cc)
@@ -168,19 +169,24 @@
         rs[layer] = jnp.broadcast_to(rstd, (BLK, 128))
         return (hat * gain + shift).astype(BF16)
 
-    def norm_grad(d_out, gain, xh, rs, layer, gain_row):
+    def norm_grad(d_out, gain, xh, rs, layer, rows):
         hat = xh[layer]
         rstd = rs[layer][:, :1]
-        sg[layer, gain_row:gain_row + 1, :] = jnp.sum(d_out * hat, axis=0, keepdims=True)
-        sg[layer, gain_row + 1:gain_row + 2, :] = jnp.sum(d_out, axis=0, keepdims=True)
+        rows[layer, 0:1, :] = jnp.sum(d_out * hat, axis=0, keepdims=True)
+        rows[layer, 1:2, :] = jnp.sum(d_out, axis=0, keepdims=True)
         d_hat = d_out * gain
         m1 = jnp.mean(d_hat, axis=-1, keepdims=True)
         m2 = jnp.mean(d_hat * hat, axis=-1, keepdims=True)
         return rstd * (d_hat - m1 - hat * m2)
 
-    def small_copies(layer):
-        return [remote(sg.at[layer], sgr.at[layer, i], gsem.at[layer, 0, i], gsem.at[layer, 1, i], dev)
+    def small_copies(kind, layer):
+        src, dst = ((sg1, sgr1), (sg2, sgr2))[kind]
+        return [remote(src.at[layer], dst.at[layer, i], gsem.at[kind, layer, 0, i], gsem.at[kind, layer, 1, i], dev)
                 for i, dev in enumerate((sib, cross, diag))]
+
+    def small_start(kind, layer):
+        for copy in small_copies(kind, layer):
+            copy.start()
 
     load_w(0, 0)
     barrier = pltpu.get_barrier_semaphore()
@@ -249,15 +255,15 @@
         @pl.when(first)
         def _():
             load_w(3, 0)
-        @pl.when(first)
-        def _():
-            ag_relay(dm_g, N_LAYERS - 1, 1)
-
         @pl.when(last)
         def _():
             wait_w(3, N_LAYERS - 1)
         rs_send(0, lambda c: mm(attn[layer], wo[:, chunk(c)]))
         dact_early(layer, 0, 2)
+
+        @pl.when(first)
+        def _():
+            ag_relay(dm_g, N_LAYERS - 1, 1)
         rs_finish(0)
 
         @pl.when(first)
@@ -303,7 +309,6 @@
             res[...] = res[...] + own[0] + bias_ref[0, 1:2]
 
     dres[...] = dy_ref[0].astype(F32)
-    sg[...] = jnp.zeros_like(sg)
 
     @pl.loop(0, N_LAYERS)
     def _(step):
@@ -311,7 +316,7 @@
         top = step == 0
         low = step == N_LAYERS - 1
         lnp = ln_ref[layer]
-        sg[layer, 5:6, :] = jnp.sum(dres[...], axis=0, keepdims=True)
+        sg2[layer, 3:4, :] = jnp.sum(dres[...], axis=0, keepdims=True)
         @pl.when(low)
         def _():
             dm_g[0, me] = dres[...].astype(BF16)
@@ -330,6 +335,8 @@
 
         @pl.when(low)
         def _():
+            small_start(0, N_LAYERS - 1)
+            small_start(1, N_LAYERS - 1)
             wait_w(2, 0)
         rs_send(0, lambda c: mm_nt(wu[chunk(c), :], dpre[layer]).T)
 
@@ -339,9 +346,9 @@
             rs_send(2, lambda c: mm(act[N_LAYERS - 1], wd[:, chunk(c)]))
             load_w(3, 0)
         rs_finish(0)
-        dres[...] = dres[...] + norm_grad(own[0], lnp[2:3], xh2, rs2, layer, 2)
-
-        sg[layer, 4:5, :] = jnp.sum(dres[...], axis=0, keepdims=True)
+        dres[...] = dres[...] + norm_grad(own[0], lnp[2:3], xh2, rs2, layer, sg2)
+
+        sg2[layer, 2:3, :] = jnp.sum(dres[...], axis=0, keepdims=True)
         da_g[layer, me] = dres[...].astype(BF16)
         ag_start(da_g, layer)
         acct[0:ATT, :] = jnp.zeros((ATT, SEQ), F32)
@@ -364,8 +371,7 @@
 
         @pl.when(low)
         def _():
-            for copy in small_copies(N_LAYERS - 1):
-                copy.start()
+            small_start(1, 0)
 
         for hd in range(HEADS):
             q = qkv[layer, :, hd * HD:(hd + 1) * HD]
@@ -392,21 +398,21 @@
         @pl.when(top)
         def _():
             load_w(0, 0)
-        dres[...] = dres[...] + norm_grad(own[0], lnp[0:1], xh1, rs1, layer, 0)
-
-    for copy in small_copies(0):
-        copy.start()
+        dres[...] = dres[...] + norm_grad(own[0], lnp[0:1], xh1, rs1, layer, sg1)
+
+    small_start(0, 0)
     xg_ref[...] = dres[...].astype(BF16)
-    for layer in reversed(range(N_LAYERS)):
-        for copy in small_copies(layer):
+    for kind, layer in ((0, 1), (1, 1), (1, 0), (0, 0)):
+        src, dst, out = ((sg1, sgr1, small1_ref), (sg2, sgr2, small2_ref))[kind]
+        for copy in small_copies(kind, layer):
             copy.wait()
-        small_ref[layer] = (sg[layer] + sgr[layer, 0]) + (sgr[layer, 1] + sgr[layer, 2])
+        out[layer] = (src[layer] + dst[layer, 0]) + (dst[layer, 1] + dst[layer, 2])
     for layer in range(N_LAYERS):
         for i, (src, dst) in enumerate(outs):
             out_copy(i, src, dst, layer).wait()
 
 
-def grads_kernel(y_in, xg_in, small_in, bupg_in, h_h, h2_h, dm_h, da_h, a_h, act_h, dpre_h, dqkv_h,
+def grads_kernel(y_in, xg_in, small1_in, small2_in, bupg_in, h_h, h2_h, dm_h, da_h, a_h, act_h, dpre_h, dqkv_h,
                  y_o, xg_o, lng_o, biasg_o, wqkv_o, wo_o, wu_o, bupg_o, wd_o,
                  h, h2, dm, da, attn, act, dpre, dqkv, big, qbuf, obuf, isem, bsem, qsem, osem):
     ins = [(dm_h, dm), (act_h, act), (h2_h, h2), (dpre_h, dpre), (da_h, da), (a_h, attn), (h_h, h), (dqkv_h, dqkv)]
@@ -425,18 +431,30 @@
     prefetch(1)
     y_o[...] = y_in[...]
     xg_o[...] = xg_in[...]
-    lng_o[...] = small_in[:, 0:4, :]
-    biasg_o[...] = small_in[:, 4:6, :]
+    lng_o[:, 0:2, :] = small1_in[...]
+    lng_o[:, 2:4, :] = small2_in[:, 0:2, :]
+    biasg_o[...] = small2_in[:, 2:4, :]
     bupg_o[...] = bupg_in[...]
 
-    def big_copy(dst, layer, c, slot):
-        return pltpu.make_async_copy(big.at[slot], dst.at[layer, chunk(c)], bsem.at[slot])
-
-    def q_copy(layer, c, slot):
-        return pltpu.make_async_copy(qbuf.at[slot], wqkv_o.at[layer, :, chunk(c), :], qsem.at[slot])
-
-    def o_copy(layer, c):
-        return pltpu.make_async_copy(obuf.at[c], wo_o.at[layer, pl.ds(c * (ATT // 2), ATT // 2)], osem.at[c])
+    def big_copies(dst, layer, c, slot):
+        return [pltpu.make_async_copy(big.at[slot, pl.ds(r * 128, 128)], dst.at[layer, pl.ds(pl.multiple_of(c * C + r * 128, 128), 128)],
+                                      bsem.at[slot, r]) for r in range(C // 128)]
+
+    def q_copies(layer, c, slot):
+        return [pltpu.make_async_copy(qbuf.at[slot, pl.ds(3 * j, 3)], wqkv_o.at[layer, pl.ds(3 * j, 3), chunk(c), :], qsem.at[slot, j])
+                for j in range(HEADS)]
+
+    def o_copies(layer, c):
+        return [pltpu.make_async_copy(obuf.at[c, pl.ds(r * 160, 160)], wo_o.at[layer, pl.ds(c * (ATT // 2) + r * 160, 160)], osem.at[c, r])
+                for r in range(2)]
+
+    def start(copies):
+        for copy in copies:
+            copy.start()
+
+    def wait(copies):
+        for copy in copies:
+            copy.wait()
 
     for step, layer in enumerate(reversed(range(N_LAYERS))):
         for w, (dst, left, right) in enumerate(((wd_o, act, dm), (wu_o, h2, dpre))):
@@ -447,25 +465,25 @@
 
             @pl.loop(0, NC)
             def _(c):
-                slot = lax.rem(base + c, 3)
-
-                @pl.when(base + c >= 3)
+                slot = lax.rem(base + c, SLOTS)
+
+                @pl.when(base + c >= SLOTS)
                 def _():
-                    big_copy(dst, layer, c, slot).wait()
+                    wait(big_copies(dst, layer, c, slot))
                 lt = left[layer, :, chunk(c)].T
                 for n in range(0, D, C):
                     big[slot, :, n:n + C] = mm(lt, right[layer, :, n:n + C]).astype(BF16)
-                big_copy(dst, layer, c, slot).start()
+                start(big_copies(dst, layer, c, slot))
         in_copy(4, layer).wait()
         in_copy(5, layer).wait()
         prefetch(4 * step + 4)
         for c in range(2):
             if step > 0:
-                o_copy(layer, c).wait()
+                wait(o_copies(layer, c))
             lt = attn[layer, :, :].T[c * (ATT // 2):(c + 1) * (ATT // 2)]
             for n in range(0, D, C):
                 obuf[c, :, n:n + C] = mm(lt, da[layer, :, n:n + C]).astype(BF16)
-            o_copy(layer, c).start()
+            start(o_copies(layer, c))
         in_copy(6, layer).wait()
         in_copy(7, layer).wait()
         prefetch(4 * step + 5)
@@ -477,18 +495,19 @@
 
             @pl.when(qbase + c >= 3)
             def _():
-                q_copy(layer, c, slot).wait()
+                wait(q_copies(layer, c, slot))
             lt = h[layer, :, chunk(c)].T
             for n in range(0, QKV, 3 * HD):
                 vals = mm(lt, dqkv[layer, :, n:n + 3 * HD]).astype(BF16)
                 for j in range(3):
                     qbuf[slot, n // HD + j] = vals[:, j * HD:(j + 1) * HD]
-            q_copy(layer, c, slot).start()
+            start(q_copies(layer, c, slot))
+    for slot in range(SLOTS):
+        wait(big_copies(wu_o, 0, 0, slot))
     for slot in range(3):
-        big_copy(wu_o, 0, 0, slot).wait()
-        q_copy(0, 0, slot).wait()
+        wait(q_copies(0, 0, slot))
     for c in range(2):
-        o_copy(0, c).wait()
+        wait(o_copies(0, c))
 
 
 def solution(mesh):
@@ -504,12 +523,12 @@
         chain_out = pl.pallas_call(
             chain_kernel,
             name='chain',
-            out_shape=(sds((BLK, D), BF16), sds((BLK, D), BF16), sds((N_LAYERS, 8, D), F32), sds((N_LAYERS, FF), F32),
+            out_shape=(sds((BLK, D), BF16), sds((BLK, D), BF16), sds((N_LAYERS, 2, D), F32), sds((N_LAYERS, 4, D), F32), sds((N_LAYERS, FF), F32),
                        sds(gath, BF16), sds(gath, BF16), sds(gath, BF16), sds(gath, BF16),
                        sds((N_LAYERS, SEQ, ATT), BF16), sds((N_LAYERS, SEQ, FF), BF16), sds((N_LAYERS, SEQ, FF), BF16),
                        sds((N_LAYERS, SEQ, QKV), BF16)),
             in_specs=[vmem] * 5 + [hbm] * 4,
-            out_specs=tuple([vmem] * 4 + [hbm] * 8),
+            out_specs=tuple([vmem] * 5 + [hbm] * 8),
             scratch_shapes=[
                 pltpu.VMEM((D, QKV), BF16), pltpu.VMEM((ATT, D), BF16), pltpu.VMEM((D, FF), BF16), pltpu.VMEM((FF, D), BF16),
                 pltpu.VMEM(gath, BF16), pltpu.VMEM(gath, BF16), pltpu.VMEM(gath, BF16), pltpu.VMEM(gath, BF16),
@@ -521,12 +540,12 @@
                 pltpu.VMEM((BLK, D), F32), pltpu.VMEM((BLK, D), F32), pltpu.VMEM((SEQ, D), F32), pltpu.VMEM((D, SEQ), F32),
                 pltpu.VMEM((2, 2, 2, BLK, D), F32), pltpu.VMEM((2, BLK, D), F32), pltpu.VMEM((3, 2, BLK, D), F32),
                 pltpu.VMEM((3, BLK, D), BF16), pltpu.VMEM((2, BLK, D), BF16),
-                pltpu.VMEM((N_LAYERS, 8, D), F32), pltpu.VMEM((N_LAYERS, 3, 8, D), F32),
-                dma((4, 3 * HEADS)), dma((8, N_LAYERS)), dma((2, 6, NC)), dma((3, 4, NC)), dma((N_LAYERS, 2, 3)),
+                pltpu.VMEM((N_LAYERS, 2, D), F32), pltpu.VMEM((N_LAYERS, 4, D), F32), pltpu.VMEM((N_LAYERS, 3, 2, D), F32), pltpu.VMEM((N_LAYERS, 3, 4, D), F32),
+                dma((4, 3 * HEADS)), dma((8, N_LAYERS)), dma((2, 6, NC)), dma((3, 4, NC)), dma((2, N_LAYERS, 2, 3)),
             ],
             compiler_params=pltpu.CompilerParams(collective_id=0, has_side_effects=True, vmem_limit_bytes=VMEM_ALL),
         )(x_loc, dy_loc, ln_par, bias_d, b_up, wqkv_t, wo_t, w_up, w_down)
-        y_loc, xg_loc, small, bupg, h, h2, dm, da, attn, act, dpre, dqkv = chain_out
+        y_loc, xg_loc, small1, small2, bupg, h, h2, dm, da, attn, act, dpre, dqkv = chain_out
         flat = (N_LAYERS, SEQ, D)
         y_out, x_grad, lng, biasg, wqkv_g, wo_g, wu_g, bupg_o, wd_g = pl.pallas_call(
             grads_kernel,
@@ -534,17 +553,17 @@
             out_shape=(sds((BLK, D), BF16), sds((BLK, D), BF16), sds((N_LAYERS, 4, D), F32), sds((N_LAYERS, 2, D), F32),
                        sds((N_LAYERS, 3 * HEADS, D, HD), BF16), sds((N_LAYERS, ATT, D), BF16), sds((N_LAYERS, D, FF), BF16),
                        sds((N_LAYERS, FF), F32), sds((N_LAYERS, FF, D), BF16)),
-            in_specs=[vmem] * 4 + [hbm] * 8,
+            in_specs=[vmem] * 5 + [hbm] * 8,
             out_specs=(vmem, vmem, vmem, vmem, hbm, hbm, hbm, vmem, hbm),
             scratch_shapes=[
                 pltpu.VMEM(flat, BF16), pltpu.VMEM(flat, BF16), pltpu.VMEM(flat, BF16), pltpu.VMEM(flat, BF16),
                 pltpu.VMEM((N_LAYERS, SEQ, ATT), BF16), pltpu.VMEM((N_LAYERS, SEQ, FF), BF16), pltpu.VMEM((N_LAYERS, SEQ, FF), BF16),
                 pltpu.VMEM((N_LAYERS, SEQ, QKV), BF16),
-                pltpu.VMEM((3, C, D), BF16), pltpu.VMEM((3, 3 * HEADS, C, HD), BF16), pltpu.VMEM((2, ATT // 2, D), BF16),
-                dma((8, N_LAYERS)), dma((3,)), dma((3,)), dma((2,)),
+                pltpu.VMEM((SLOTS, C, D), BF16), pltpu.VMEM((3, 3 * HEADS, C, HD), BF16), pltpu.VMEM((2, ATT // 2, D), BF16),
+                dma((8, N_LAYERS)), dma((SLOTS, C // 128)), dma((3, HEADS)), dma((2, 2)),
             ],
             compiler_params=pltpu.CompilerParams(vmem_limit_bytes=VMEM_ALL),
-        )(y_loc, xg_loc, small, bupg, h.reshape(flat), h2.reshape(flat), dm.reshape(flat), da.reshape(flat), attn, act, dpre, dqkv)
+        )(y_loc, xg_loc, small1, small2, bupg, h.reshape(flat), h2.reshape(flat), dm.reshape(flat), da.reshape(flat), attn, act, dpre, dqkv)
         wqkv_g = jnp.transpose(wqkv_g.reshape(N_LAYERS, 3, HEADS, D, HD), (0, 3, 1, 2, 4))
         return (y_out[None], x_grad[None], lng, biasg, wqkv_g, wo_g.reshape(N_LAYERS, HEADS, HD, D), wu_g, bupg_o, wd_g)
 

time: 169 us -> 163 us (0.964)
  Pallas kernels: 168 us -> 162 us
    pallas_call x1, Pallas kernels: 137 us -> 130 us  [device_step(): pl.pallas_call(chain_kernel, name='chain', out_shape=(sds((BLK, D), BF16)...]
where the time goes in v2:
time: 163 us
  Pallas kernels  162 us (99%)
    pallas_call x1, Pallas kernels, device_step(): pl.pallas_call(chain_kernel, name='chain', out_shape=(sds((BLK, D), BF16)...  130 us
    pallas_call x1, Pallas kernels, device_step(): pl.pallas_call(grads_kernel, name='grads', out_shape=(sds((BLK, D), BF16)...  31.9 us

profile of v2, /device:TPU:0, one launch (start us, length us, event | category | flops | bytes accessed | tf_op | source)
XLA Modules:
  0.0 162.8 jit_solution(5654204608473493336)
XLA Ops:
  0.6 130.3 %chain.1 = (bf16[32,2560]{1,0:T(8,128)(2,1)}, bf16[32,2560]{1,0:T(8,128)(2,1)}, f32[2,2,2560]{2,1,0:T(2,128)}, f32[2,4,2560]{2,1,0:T(4,128)}, f32[2,2560]{1,0:T(...) custom-call(bf16[1,32,2560]{2,1,0:T(8,128)(2,1)} %x_ref.1, ...), custom_call_target="tpu_custom_call" | custom-call | tf_op jit(solution)/shard_map/chain/pallas_call | solution.py:523
  131.0 31.9 %grads.1 = (bf16[32,2560]{1,0:T(8,128)(2,1)}, bf16[32,2560]{1,0:T(8,128)(2,1)}, f32[2,4,2560]{2,1,0:T(4,128)}, f32[2,2,2560]{2,1,0:T(2,128)}, bf16[2,15,2560,128...) custom-call(bf16[32,2560]{1,0:T(8,128)(2,1)} %get-tuple-element.31.y, ...), custom_call_target="tpu_custom_call" | custom-call | tf_op jit(solution)/shard_map/grads/pallas_call | solution.py:550

commit v3 on v2

--- a/solution.py
+++ b/solution.py
@@ -13,6 +13,9 @@
 C = 512
 NC = D // C
 SLOTS = 4
+CA = 256
+NA = D // CA
+ND = 2
 SCALE = HD ** -0.5
 GELU_K = 0.7978845608028654
 GELU_C = 0.044715
@@ -25,10 +28,6 @@
 
 def mm_nt(a, b):
     return lax.dot_general(a, b, (((1,), (1,)), ((), ())), preferred_element_type=F32)
-
-
-def mm_tn(a, b):
-    return mm(a.T, b)
 
 
 def chunk(c, size=C):
@@ -72,43 +71,61 @@
 
     outs = [(h_g, h_o), (h2_g, h2_o), (dm_g, dm_o), (da_g, da_o), (attn, a_o), (act, act_o), (dpre, dpre_o), (dqkv, dqkv_o)]
 
+    def ag_mine(g, layer, c, k, i, dev):
+        mine = g.at[layer, me, :, chunk(c, CA)]
+        return remote(mine, mine, agsem.at[k, i, c], agsem.at[k, i + 1, c], dev)
+
     def ag_side(g, layer, c, k=0):
-        mine = g.at[layer, me, :, chunk(c)]
-        return remote(mine, mine, agsem.at[k, 0, c], agsem.at[k, 1, c], sib)
+        return ag_mine(g, layer, c, k, 0, sib)
 
     def ag_across(g, layer, c, k=0):
-        mine = g.at[layer, me, :, chunk(c)]
-        return remote(mine, mine, agsem.at[k, 2, c], agsem.at[k, 3, c], cross)
+        return ag_mine(g, layer, c, k, 2, cross)
 
     def ag_forward(g, layer, c, k=0):
-        theirs = g.at[layer, cross, :, chunk(c)]
+        theirs = g.at[layer, cross, :, chunk(c, CA)]
         return remote(theirs, theirs, agsem.at[k, 4, c], agsem.at[k, 5, c], sib)
 
+    def ag_direct(g, layer, c, k=0):
+        return ag_mine(g, layer, c, k, 4, diag)
+
     def ag_relay(g, layer, k):
-        @pl.loop(0, NC)
+        @pl.loop(0, NA)
         def _(c):
             ag_across(g, layer, c, k).wait_recv()
-            ag_forward(g, layer, c, k).start()
+
+            @pl.when(c < NA - ND)
+            def _():
+                ag_forward(g, layer, c, k).start()
 
     def ag_finish(g, layer, k):
-        @pl.loop(0, NC)
+        @pl.loop(0, NA)
         def _(c):
             ag_side(g, layer, c, k).wait()
             ag_forward(g, layer, c, k).wait()
             ag_across(g, layer, c, k).wait_send()
 
     def ag_start(g, layer, k=0):
-        for c in range(NC):
+        @pl.loop(0, NA)
+        def _(c):
             ag_across(g, layer, c, k).start()
-        for c in range(NC):
+
+            @pl.when(c >= NA - ND)
+            def _():
+                ag_direct(g, layer, c, k).start()
+
+        @pl.loop(0, NA)
+        def _(c):
             ag_side(g, layer, c, k).start()
 
-    def ag_consume(g, layer, compute, lag=2):
-        @pl.loop(0, NC + lag)
-        def _(c):
-            @pl.when(c < NC)
+    def ag_consume(g, layer, compute, lag=3):
+        @pl.loop(0, NA + lag)
+        def _(c):
+            @pl.when(c < NA)
             def _():
                 ag_across(g, layer, c).wait_recv()
+
+            @pl.when(c < NA - ND)
+            def _():
                 ag_forward(g, layer, c).start()
 
             @pl.when(c >= lag)
@@ -118,7 +135,7 @@
                 ag_forward(g, layer, cc).wait_recv()
                 compute(cc)
 
-        @pl.loop(0, NC)
+        @pl.loop(0, NA)
         def _(c):
             ag_side(g, layer, c).wait_send()
             ag_across(g, layer, c).wait_send()
@@ -200,8 +217,8 @@
     causal = row_id >= col_id
 
     def dact_chunk(c):
-        g = dm_g[0, :, :, chunk(c)].reshape(SEQ, C)
-        acct[...] += mm_nt(wd[:, chunk(c)], g)
+        g = dm_g[0, :, :, chunk(c, CA)].reshape(SEQ, CA)
+        acct[...] += mm_nt(wd[:, chunk(c, CA)], g)
 
     def dact_early(layer, lo, hi):
         @pl.when(layer == N_LAYERS - 1)
@@ -209,6 +226,22 @@
             @pl.loop(lo, hi)
             def _(c):
                 acct[chunk(c), :] = mm_nt(wd[chunk(c), :], dm_g[N_LAYERS - 1].reshape(SEQ, D))
+
+    def act_chunk(layer, c):
+        pre = acc[:, chunk(c)] + bup_ref[layer:layer + 1, chunk(c)]
+        t = jnp.tanh(pre * (GELU_K + (GELU_K * GELU_C) * (pre * pre)))
+        act[layer, :, chunk(c)] = (pre * (0.5 + 0.5 * t)).astype(BF16)
+
+    def slope_chunk(layer, c):
+        pre = acc[:, chunk(c)] + bup_ref[layer:layer + 1, chunk(c)]
+        sq = pre * pre
+        t = jnp.tanh(pre * (GELU_K + (GELU_K * GELU_C) * sq))
+        return (0.5 + 0.5 * t) + (pre * (1.0 - t * t)) * (0.5 * GELU_K + (1.5 * GELU_K * GELU_C) * sq)
+
+    def dpre_chunk(layer, c, slope):
+        d_pre = acct[chunk(c), :].T * slope
+        bupg_ref[layer:layer + 1, chunk(c)] = jnp.sum(d_pre, axis=0, keepdims=True)
+        dpre[layer, :, chunk(c)] = d_pre.astype(BF16)
 
     @pl.loop(0, N_LAYERS)
     def _(layer):
@@ -226,9 +259,9 @@
             load_w(2, 0)
 
         def qkv_chunk(c):
-            h = h_g[layer, :, :, chunk(c)].reshape(SEQ, C)
+            h = h_g[layer, :, :, chunk(c, CA)].reshape(SEQ, CA)
             for n in range(0, QKV, 640):
-                acc[:, n:n + 640] += mm(h, wq[chunk(c), n:n + 640])
+                acc[:, n:n + 640] += mm(h, wq[chunk(c, CA), n:n + 640])
         ag_consume(h_g, layer, qkv_chunk)
         out_copy(0, h_g, h_o, layer).start()
 
@@ -280,9 +313,9 @@
         dact_early(layer, 2, NC)
 
         def up_chunk(c):
-            h = h2_g[layer, :, :, chunk(c)].reshape(SEQ, C)
+            h = h2_g[layer, :, :, chunk(c, CA)].reshape(SEQ, CA)
             for n in range(0, FF, C):
-                acc[:, n:n + C] += mm(h, wu[chunk(c), n:n + C])
+                acc[:, n:n + C] += mm(h, wu[chunk(c, CA), n:n + C])
         ag_consume(h2_g, layer, up_chunk)
         out_copy(1, h2_g, h2_o, layer).start()
 
@@ -290,24 +323,26 @@
         def _():
             load_w(2, 1)
 
-        @pl.loop(0, FF // C)
-        def _(c):
-            pre = acc[:, chunk(c)] + bup_ref[pl.ds(layer, 1), chunk(c)]
-            sq = pre * pre
-            t = jnp.tanh(GELU_K * (pre + GELU_C * (sq * pre)))
-            cdf = 0.5 * (1.0 + t)
-            act[layer, :, chunk(c)] = (pre * cdf).astype(BF16)
-            gp[layer, :, chunk(c)] = cdf + 0.5 * pre * (1.0 - t * t) * (GELU_K * (1.0 + 3.0 * GELU_C * sq))
-        out_copy(5, act, act_o, layer).start()
-
         @pl.when(first)
         def _():
+            @pl.loop(0, FF // C)
+            def _(c):
+                act_chunk(0, c)
+            out_copy(5, act, act_o, 0).start()
             wait_w(3, 0)
             rs_send(1, lambda c: mm(act[0], wd[:, chunk(c)]))
+
+            @pl.loop(0, FF // C)
+            def _(c):
+                gp[:, chunk(c)] = slope_chunk(0, c)
             rs_finish(1)
             load_w(3, 1)
             res[...] = res[...] + own[0] + bias_ref[0, 1:2]
 
+    @pl.loop(0, FF // C)
+    def _(c):
+        dpre_chunk(N_LAYERS - 1, c, slope_chunk(N_LAYERS - 1, c))
+    out_copy(6, dpre, dpre_o, N_LAYERS - 1).start()
     dres[...] = dy_ref[0].astype(F32)
 
     @pl.loop(0, N_LAYERS)
@@ -326,12 +361,12 @@
             ag_consume(dm_g, 0, dact_chunk)
             out_copy(2, dm_g, dm_o, 0).start()
 
-        @pl.loop(0, FF // C)
-        def _(c):
-            d_pre = acct[chunk(c), :].T * gp[layer, :, chunk(c)]
-            bupg_ref[pl.ds(layer, 1), chunk(c)] = jnp.sum(d_pre, axis=0, keepdims=True)
-            dpre[layer, :, chunk(c)] = d_pre.astype(BF16)
-        out_copy(6, dpre, dpre_o, layer).start()
+        @pl.when(low)
+        def _():
+            @pl.loop(0, FF // C)
+            def _(c):
+                dpre_chunk(0, c, gp[:, chunk(c)])
+            out_copy(6, dpre, dpre_o, 0).start()
 
         @pl.when(low)
         def _():
@@ -343,6 +378,11 @@
         @pl.when(top)
         def _():
             load_w(2, 0)
+
+            @pl.loop(0, FF // C)
+            def _(c):
+                act_chunk(N_LAYERS - 1, c)
+            out_copy(5, act, act_o, N_LAYERS - 1).start()
             rs_send(2, lambda c: mm(act[N_LAYERS - 1], wd[:, chunk(c)]))
             load_w(3, 0)
         rs_finish(0)
@@ -358,8 +398,8 @@
             wait_w(1, 0)
 
         def dattn_chunk(c):
-            g = da_g[layer, :, :, chunk(c)].reshape(SEQ, C)
-            acct[0:ATT, :] += mm_nt(wo[:, chunk(c)], g)
+            g = da_g[layer, :, :, chunk(c, CA)].reshape(SEQ, CA)
+            acct[0:ATT, :] += mm_nt(wo[:, chunk(c, CA)], g)
         ag_consume(da_g, layer, dattn_chunk)
         out_copy(3, da_g, da_o, layer).start()
 
@@ -414,7 +454,7 @@
 
 def grads_kernel(y_in, xg_in, small1_in, small2_in, bupg_in, h_h, h2_h, dm_h, da_h, a_h, act_h, dpre_h, dqkv_h,
                  y_o, xg_o, lng_o, biasg_o, wqkv_o, wo_o, wu_o, bupg_o, wd_o,
-                 h, h2, dm, da, attn, act, dpre, dqkv, big, qbuf, obuf, isem, bsem, qsem, osem):
+                 h, h2, dm, da, attn, act, dpre, dqkv, big, qbuf, obuf, y_v, xg_v, small1_v, small2_v, bupg_v, lng_v, biasg_v, isem, bsem, qsem, osem, psem):
     ins = [(dm_h, dm), (act_h, act), (h2_h, h2), (dpre_h, dpre), (da_h, da), (a_h, attn), (h_h, h), (dqkv_h, dqkv)]
 
     def in_copy(i, layer):
@@ -429,12 +469,12 @@
 
     prefetch(0)
     prefetch(1)
-    y_o[...] = y_in[...]
-    xg_o[...] = xg_in[...]
-    lng_o[:, 0:2, :] = small1_in[...]
-    lng_o[:, 2:4, :] = small2_in[:, 0:2, :]
-    biasg_o[...] = small2_in[:, 2:4, :]
-    bupg_o[...] = bupg_in[...]
+    small_in = [pltpu.make_async_copy(src, dst, psem.at[i]) for i, (src, dst) in enumerate(
+        ((y_in, y_v), (xg_in, xg_v), (small1_in, small1_v), (small2_in, small2_v), (bupg_in, bupg_v)))]
+    small_out = [pltpu.make_async_copy(src, dst, psem.at[i]) for i, (src, dst) in enumerate(
+        ((y_v, y_o), (xg_v, xg_o), (lng_v, lng_o), (biasg_v, biasg_o), (bupg_v, bupg_o)))]
+    for copy in small_in:
+        copy.start()
 
     def big_copies(dst, layer, c, slot):
         return [pltpu.make_async_copy(big.at[slot, pl.ds(r * 128, 128)], dst.at[layer, pl.ds(pl.multiple_of(c * C + r * 128, 128), 128)],
@@ -474,6 +514,14 @@
                 for n in range(0, D, C):
                     big[slot, :, n:n + C] = mm(lt, right[layer, :, n:n + C]).astype(BF16)
                 start(big_copies(dst, layer, c, slot))
+        if step == 0:
+            for copy in small_in:
+                copy.wait()
+            lng_v[:, 0:2, :] = small1_v[...]
+            lng_v[:, 2:4, :] = small2_v[:, 0:2, :]
+            biasg_v[...] = small2_v[:, 2:4, :]
+            for copy in small_out:
+                copy.start()
         in_copy(4, layer).wait()
         in_copy(5, layer).wait()
         prefetch(4 * step + 4)
@@ -502,6 +550,8 @@
                 for j in range(3):
                     qbuf[slot, n // HD + j] = vals[:, j * HD:(j + 1) * HD]
             start(q_copies(layer, c, slot))
+    for copy in small_out:
+        copy.wait()
     for slot in range(SLOTS):
         wait(big_copies(wu_o, 0, 0, slot))
     for slot in range(3):
@@ -533,7 +583,7 @@
                 pltpu.VMEM((D, QKV), BF16), pltpu.VMEM((ATT, D), BF16), pltpu.VMEM((D, FF), BF16), pltpu.VMEM((FF, D), BF16),
                 pltpu.VMEM(gath, BF16), pltpu.VMEM(gath, BF16), pltpu.VMEM(gath, BF16), pltpu.VMEM(gath, BF16),
                 pltpu.VMEM((N_LAYERS, SEQ, QKV), BF16), pltpu.VMEM((N_LAYERS, HEADS, SEQ, SEQ), BF16),
-                pltpu.VMEM((N_LAYERS, SEQ, ATT), BF16), pltpu.VMEM((N_LAYERS, SEQ, FF), BF16), pltpu.VMEM((N_LAYERS, SEQ, FF), F32),
+                pltpu.VMEM((N_LAYERS, SEQ, ATT), BF16), pltpu.VMEM((N_LAYERS, SEQ, FF), BF16), pltpu.VMEM((SEQ, FF), F32),
                 pltpu.VMEM((N_LAYERS, SEQ, FF), BF16), pltpu.VMEM((N_LAYERS, SEQ, QKV), BF16),
                 pltpu.VMEM((N_LAYERS, BLK, D), F32), pltpu.VMEM((N_LAYERS, BLK, D), F32),
                 pltpu.VMEM((N_LAYERS, BLK, 128), F32), pltpu.VMEM((N_LAYERS, BLK, 128), F32),
@@ -541,7 +591,7 @@
                 pltpu.VMEM((2, 2, 2, BLK, D), F32), pltpu.VMEM((2, BLK, D), F32), pltpu.VMEM((3, 2, BLK, D), F32),
                 pltpu.VMEM((3, BLK, D), BF16), pltpu.VMEM((2, BLK, D), BF16),
                 pltpu.VMEM((N_LAYERS, 2, D), F32), pltpu.VMEM((N_LAYERS, 4, D), F32), pltpu.VMEM((N_LAYERS, 3, 2, D), F32), pltpu.VMEM((N_LAYERS, 3, 4, D), F32),
-                dma((4, 3 * HEADS)), dma((8, N_LAYERS)), dma((2, 6, NC)), dma((3, 4, NC)), dma((2, N_LAYERS, 2, 3)),
+                dma((4, 3 * HEADS)), dma((8, N_LAYERS)), dma((2, 6, NA)), dma((3, 4, NC)), dma((2, N_LAYERS, 2, 3)),
             ],
             compiler_params=pltpu.CompilerParams(collective_id=0, has_side_effects=True, vmem_limit_bytes=VMEM_ALL),
         )(x_loc, dy_loc, ln_par, bias_d, b_up, wqkv_t, wo_t, w_up, w_down)
@@ -553,14 +603,16 @@
             out_shape=(sds((BLK, D), BF16), sds((BLK, D), BF16), sds((N_LAYERS, 4, D), F32), sds((N_LAYERS, 2, D), F32),
                        sds((N_LAYERS, 3 * HEADS, D, HD), BF16), sds((N_LAYERS, ATT, D), BF16), sds((N_LAYERS, D, FF), BF16),
                        sds((N_LAYERS, FF), F32), sds((N_LAYERS, FF, D), BF16)),
-            in_specs=[vmem] * 5 + [hbm] * 8,
-            out_specs=(vmem, vmem, vmem, vmem, hbm, hbm, hbm, vmem, hbm),
+            in_specs=[hbm] * 13,
+            out_specs=tuple([hbm] * 9),
             scratch_shapes=[
                 pltpu.VMEM(flat, BF16), pltpu.VMEM(flat, BF16), pltpu.VMEM(flat, BF16), pltpu.VMEM(flat, BF16),
                 pltpu.VMEM((N_LAYERS, SEQ, ATT), BF16), pltpu.VMEM((N_LAYERS, SEQ, FF), BF16), pltpu.VMEM((N_LAYERS, SEQ, FF), BF16),
                 pltpu.VMEM((N_LAYERS, SEQ, QKV), BF16),
                 pltpu.VMEM((SLOTS, C, D), BF16), pltpu.VMEM((3, 3 * HEADS, C, HD), BF16), pltpu.VMEM((2, ATT // 2, D), BF16),
-                dma((8, N_LAYERS)), dma((SLOTS, C // 128)), dma((3, HEADS)), dma((2, 2)),
+                pltpu.VMEM((BLK, D), BF16), pltpu.VMEM((BLK, D), BF16), pltpu.VMEM((N_LAYERS, 2, D), F32), pltpu.VMEM((N_LAYERS, 4, D), F32),
+                pltpu.VMEM((N_LAYERS, FF), F32), pltpu.VMEM((N_LAYERS, 4, D), F32), pltpu.VMEM((N_LAYERS, 2, D), F32),
+                dma((8, N_LAYERS)), dma((SLOTS, C // 128)), dma((3, HEADS)), dma((2, 2)), dma((5,)),
             ],
             compiler_params=pltpu.CompilerParams(vmem_limit_bytes=VMEM_ALL),
         )(y_loc, xg_loc, small1, small2, bupg, h.reshape(flat), h2.reshape(flat), dm.reshape(flat), da.reshape(flat), attn, act, dpre, dqkv)

time: 163 us -> 165 us (1.012)
  Pallas kernels: 162 us -> 164 us
    pallas_call x1, Pallas kernels: 130 us -> 134 us  [device_step(): pl.pallas_call(chain_kernel, name='chain', out_shape=(sds((BLK, D), BF16)...]
where the time goes in v3:
time: 165 us
  Pallas kernels  164 us (99%)
    pallas_call x1, Pallas kernels, device_step(): pl.pallas_call(chain_kernel, name='chain', out_shape=(sds((BLK, D), BF16)...  134 us
    pallas_call x1, Pallas kernels, device_step(): pl.pallas_call(grads_kernel, name='grads', out_shape=(sds((BLK, D), BF16)...  30.4 us

profile of v3, /device:TPU:0, one launch (start us, length us, event | category | flops | bytes accessed | tf_op | source)
XLA Modules:
  0.0 164.7 jit_solution(8299936319961691602)
XLA Ops:
  0.6 133.7 %chain.1 = (bf16[32,2560]{1,0:T(8,128)(2,1)}, bf16[32,2560]{1,0:T(8,128)(2,1)}, f32[2,2,2560]{2,1,0:T(2,128)}, f32[2,4,2560]{2,1,0:T(4,128)}, f32[2,2560]{1,0:T(...) custom-call(bf16[1,32,2560]{2,1,0:T(8,128)(2,1)} %x_ref.1, ...), custom_call_target="tpu_custom_call" | custom-call | tf_op jit(solution)/shard_map/chain/pallas_call | solution.py:573
  134.3 30.4 %grads.1 = (bf16[32,2560]{1,0:T(8,128)(2,1)}, bf16[32,2560]{1,0:T(8,128)(2,1)}, f32[2,4,2560]{2,1,0:T(4,128)}, f32[2,2,2560]{2,1,0:T(2,128)}, bf16[2,15,2560,128...) custom-call(bf16[32,2560]{1,0:T(8,128)(2,1)} %get-tuple-element.31.y, ...), custom_call_target="tpu_custom_call" | custom-call | tf_op jit(solution)/shard_map/grads/pallas_call | solution.py:600

commit v4 on v3

--- a/solution.py
+++ b/solution.py
@@ -13,9 +13,9 @@
 C = 512
 NC = D // C
 SLOTS = 4
-CA = 256
+CA = 512
 NA = D // CA
-ND = 2
+ND = 1
 SCALE = HD ** -0.5
 GELU_K = 0.7978845608028654
 GELU_C = 0.044715
@@ -73,7 +73,7 @@
 
     def ag_mine(g, layer, c, k, i, dev):
         mine = g.at[layer, me, :, chunk(c, CA)]
-        return remote(mine, mine, agsem.at[k, i, c], agsem.at[k, i + 1, c], dev)
+        return remote(mine, mine, agsem.at[k, i, 0], agsem.at[k, i + 1, c], dev)
 
     def ag_side(g, layer, c, k=0):
         return ag_mine(g, layer, c, k, 0, sib)
@@ -83,10 +83,14 @@
 
     def ag_forward(g, layer, c, k=0):
         theirs = g.at[layer, cross, :, chunk(c, CA)]
-        return remote(theirs, theirs, agsem.at[k, 4, c], agsem.at[k, 5, c], sib)
+        return remote(theirs, theirs, agsem.at[k, 4, 0], agsem.at[k, 5, c], sib)
 
     def ag_direct(g, layer, c, k=0):
         return ag_mine(g, layer, c, k, 4, diag)
+
+    def ag_sent(g, layer, k=0):
+        for i, dev in ((0, sib), (2, cross), (4, sib)):
+            remote(g.at[layer, me], g.at[layer, me], agsem.at[k, i, 0], agsem.at[k, i + 1, 0], dev).wait_send()
 
     def ag_relay(g, layer, k):
         @pl.loop(0, NA)
@@ -100,24 +104,19 @@
     def ag_finish(g, layer, k):
         @pl.loop(0, NA)
         def _(c):
-            ag_side(g, layer, c, k).wait()
-            ag_forward(g, layer, c, k).wait()
-            ag_across(g, layer, c, k).wait_send()
+            ag_side(g, layer, c, k).wait_recv()
+            ag_forward(g, layer, c, k).wait_recv()
+        ag_sent(g, layer, k)
 
     def ag_start(g, layer, k=0):
-        @pl.loop(0, NA)
-        def _(c):
+        for c in range(NA):
             ag_across(g, layer, c, k).start()
-
-            @pl.when(c >= NA - ND)
-            def _():
+            if c >= NA - ND:
                 ag_direct(g, layer, c, k).start()
-
-        @pl.loop(0, NA)
-        def _(c):
+        for c in range(NA):
             ag_side(g, layer, c, k).start()
 
-    def ag_consume(g, layer, compute, lag=3):
+    def ag_consume(g, layer, compute, lag=2):
         @pl.loop(0, NA + lag)
         def _(c):
             @pl.when(c < NA)
@@ -135,18 +134,14 @@
                 ag_forward(g, layer, cc).wait_recv()
                 compute(cc)
 
-        @pl.loop(0, NA)
-        def _(c):
-            ag_side(g, layer, c).wait_send()
-            ag_across(g, layer, c).wait_send()
-            ag_forward(g, layer, c).wait_send()
+        ag_sent(g, layer)
 
     def rs_side(par, c):
         return remote(part.at[par // 2, :, 1 - core, :, chunk(c)], rr.at[par, :, :, chunk(c)],
-                      rssem.at[par, 0, c], rssem.at[par, 1, c], sib)
+                      rssem.at[par, 0, 0], rssem.at[par, 1, c], sib)
 
     def rs_across(par, c):
-        return remote(ss.at[par // 2, :, chunk(c)], xx.at[par, :, chunk(c)], rssem.at[par, 2, c], rssem.at[par, 3, c], cross)
+        return remote(ss.at[par // 2, :, chunk(c)], xx.at[par, :, chunk(c)], rssem.at[par, 2, 0], rssem.at[par, 3, 0], cross)
 
     def rs_send(par, compute, lag=2):
         buf = par // 2
@@ -170,12 +165,10 @@
                 own[buf, :, cols] = part[buf, x_id, core, :, cols] + rr[par, x_id, :, cols]
 
     def rs_finish(par):
-        @pl.loop(0, NC)
-        def _(c):
-            rs_across(par, c).wait_recv()
-            rs_side(par, c).wait_send()
-            rs_across(par, c).wait_send()
-            own[par // 2, :, chunk(c)] += xx[par, :, chunk(c)].astype(F32)
+        buf = par // 2
+        remote(part.at[buf, :, 1 - core], rr.at[par], rssem.at[par, 0, 0], rssem.at[par, 1, 0], sib).wait_send()
+        remote(ss.at[buf], xx.at[par], rssem.at[par, 2, 0], rssem.at[par, 3, 0], cross).wait()
+        return own[buf] + xx[par].astype(F32)
 
     def normed(vals, gain, shift, xh, rs, layer):
         mean_val = jnp.mean(vals, axis=-1, keepdims=True)
@@ -297,14 +290,14 @@
         @pl.when(first)
         def _():
             ag_relay(dm_g, N_LAYERS - 1, 1)
-        rs_finish(0)
+        total = rs_finish(0)
+        res[...] = res[...] + total + bias_ref[layer, 0:1]
 
         @pl.when(first)
         def _():
             load_w(1, 1)
             ag_finish(dm_g, N_LAYERS - 1, 1)
             out_copy(2, dm_g, dm_o, N_LAYERS - 1).start()
-        res[...] = res[...] + own[0] + bias_ref[layer, 0:1]
 
         h2_g[layer, me] = normed(res[...], lnp[2:3], lnp[3:4], xh2, rs2, layer)
         ag_start(h2_g, layer)
@@ -335,9 +328,9 @@
             @pl.loop(0, FF // C)
             def _(c):
                 gp[:, chunk(c)] = slope_chunk(0, c)
-            rs_finish(1)
+            total = rs_finish(1)
             load_w(3, 1)
-            res[...] = res[...] + own[0] + bias_ref[0, 1:2]
+            res[...] = res[...] + total + bias_ref[0, 1:2]
 
     @pl.loop(0, FF // C)
     def _(c):
@@ -385,8 +378,8 @@
             out_copy(5, act, act_o, N_LAYERS - 1).start()
             rs_send(2, lambda c: mm(act[N_LAYERS - 1], wd[:, chunk(c)]))
             load_w(3, 0)
-        rs_finish(0)
-        dres[...] = dres[...] + norm_grad(own[0], lnp[2:3], xh2, rs2, layer, sg2)
+        total = rs_finish(0)
+        dres[...] = dres[...] + norm_grad(total, lnp[2:3], xh2, rs2, layer, sg2)
 
         sg2[layer, 2:3, :] = jnp.sum(dres[...], axis=0, keepdims=True)
         da_g[layer, me] = dres[...].astype(BF16)
@@ -406,8 +399,8 @@
         @pl.when(top)
         def _():
             load_w(1, 0)
-            rs_finish(2)
-            y_ref[...] = (res[...] + own[1] + bias_ref[N_LAYERS - 1, 1:2]).astype(BF16)
+            total = rs_finish(2)
+            y_ref[...] = (res[...] + total + bias_ref[N_LAYERS - 1, 1:2]).astype(BF16)
 
         @pl.when(low)
         def _():
@@ -433,12 +426,12 @@
         def _():
             wait_w(0, 0)
         rs_send(1, lambda c: mm_nt(wq[chunk(c), :], dqkv[layer]).T)
-        rs_finish(1)
+        total = rs_finish(1)
 
         @pl.when(top)
         def _():
             load_w(0, 0)
-        dres[...] = dres[...] + norm_grad(own[0], lnp[0:1], xh1, rs1, layer, sg1)
+        dres[...] = dres[...] + norm_grad(total, lnp[0:1], xh1, rs1, layer, sg1)
 
     small_start(0, 0)
     xg_ref[...] = dres[...].astype(BF16)

time: 165 us -> 163 us (0.988)
  Pallas kernels: 164 us -> 162 us
    pallas_call x1, Pallas kernels: 134 us -> 131 us  [device_step(): pl.pallas_call(chain_kernel, name='chain', out_shape=(sds((BLK, D), BF16)...]
where the time goes in v4:
time: 163 us; the launch traced here: 162 us
  Pallas kernels  162 us (99%)
    pallas_call x1, Pallas kernels, device_step(): pl.pallas_call(chain_kernel, name='chain', out_shape=(sds((BLK, D), BF16)...  131 us
    pallas_call x1, Pallas kernels, device_step(): pl.pallas_call(grads_kernel, name='grads', out_shape=(sds((BLK, D), BF16)...  30.4 us

profile of v4, /device:TPU:0, one launch (start us, length us, event | category | flops | bytes accessed | tf_op | source)
XLA Modules:
  0.0 162.4 jit_solution(15412195958709777773)
XLA Ops:
  0.6 131.4 %chain.1 = (bf16[32,2560]{1,0:T(8,128)(2,1)}, bf16[32,2560]{1,0:T(8,128)(2,1)}, f32[2,2,2560]{2,1,0:T(2,128)}, f32[2,4,2560]{2,1,0:T(4,128)}, f32[2,2560]{1,0:T(...) custom-call(bf16[1,32,2560]{2,1,0:T(8,128)(2,1)} %x_ref.1, ...), custom_call_target="tpu_custom_call" | custom-call | tf_op jit(solution)/shard_map/chain/pallas_call | solution.py:566
  132.0 30.4 %grads.1 = (bf16[32,2560]{1,0:T(8,128)(2,1)}, bf16[32,2560]{1,0:T(8,128)(2,1)}, f32[2,4,2560]{2,1,0:T(4,128)}, f32[2,2,2560]{2,1,0:T(2,128)}, bf16[2,15,2560,128...) custom-call(bf16[32,2560]{1,0:T(8,128)(2,1)} %get-tuple-element.31.y, ...), custom_call_target="tpu_custom_call" | custom-call | tf_op jit(solution)/shard_map/grads/pallas_call | solution.py:593

commit v5 on v4

--- a/solution.py
+++ b/solution.py
@@ -15,7 +15,7 @@
 SLOTS = 4
 CA = 512
 NA = D // CA
-ND = 1
+ND = 0
 SCALE = HD ** -0.5
 GELU_K = 0.7978845608028654
 GELU_C = 0.044715
@@ -163,6 +163,25 @@
                 ss[buf, :, cols] = (part[buf, 1 - x_id, core, :, cols] + rr[par, 1 - x_id, :, cols]).astype(BF16)
                 rs_across(par, cc).start()
                 own[buf, :, cols] = part[buf, x_id, core, :, cols] + rr[par, x_id, :, cols]
+
+    def rs_within(par, compute):
+        @pl.loop(0, NC)
+        def _(c):
+            vals = compute(c)
+            for b in range(4):
+                part[par // 2, b // 2, b % 2, :, chunk(c)] = vals[b * BLK:(b + 1) * BLK]
+            rs_side(par, c).start()
+
+    def rs_cross(par):
+        buf = par // 2
+
+        @pl.loop(0, NC)
+        def _(c):
+            rs_side(par, c).wait_recv()
+            cols = chunk(c)
+            ss[buf, :, cols] = (part[buf, 1 - x_id, core, :, cols] + rr[par, 1 - x_id, :, cols]).astype(BF16)
+            rs_across(par, c).start()
+            own[buf, :, cols] = part[buf, x_id, core, :, cols] + rr[par, x_id, :, cols]
 
     def rs_finish(par):
         buf = par // 2
@@ -376,7 +395,7 @@
             def _(c):
                 act_chunk(N_LAYERS - 1, c)
             out_copy(5, act, act_o, N_LAYERS - 1).start()
-            rs_send(2, lambda c: mm(act[N_LAYERS - 1], wd[:, chunk(c)]))
+            rs_within(2, lambda c: mm(act[N_LAYERS - 1], wd[:, chunk(c)]))
             load_w(3, 0)
         total = rs_finish(0)
         dres[...] = dres[...] + norm_grad(total, lnp[2:3], xh2, rs2, layer, sg2)
@@ -399,8 +418,7 @@
         @pl.when(top)
         def _():
             load_w(1, 0)
-            total = rs_finish(2)
-            y_ref[...] = (res[...] + total + bias_ref[N_LAYERS - 1, 1:2]).astype(BF16)
+            rs_cross(2)
 
         @pl.when(low)
         def _():
@@ -426,11 +444,12 @@
         def _():
             wait_w(0, 0)
         rs_send(1, lambda c: mm_nt(wq[chunk(c), :], dqkv[layer]).T)
+
+        @pl.when(top)
+        def _():
+            load_w(0, 0)
+            y_ref[...] = (res[...] + rs_finish(2) + bias_ref[N_LAYERS - 1, 1:2]).astype(BF16)
         total = rs_finish(1)
-
-        @pl.when(top)
-        def _():
-            load_w(0, 0)
         dres[...] = dres[...] + norm_grad(total, lnp[0:1], xh1, rs1, layer, sg1)
 
     small_start(0, 0)

time: 163 us -> 158 us (0.969)
  Pallas kernels: 162 us -> 157 us
    pallas_call x1, Pallas kernels: 131 us -> 127 us  [device_step(): pl.pallas_call(chain_kernel, name='chain', out_shape=(sds((BLK, D), BF16)...]
where the time goes in v5:
time: 158 us
  Pallas kernels  157 us (99%)
    pallas_call x1, Pallas kernels, device_step(): pl.pallas_call(chain_kernel, name='chain', out_shape=(sds((BLK, D), BF16)...  127 us
    pallas_call x1, Pallas kernels, device_step(): pl.pallas_call(grads_kernel, name='grads', out_shape=(sds((BLK, D), BF16)...  30.4 us

profile of v5, /device:TPU:0, one launch (start us, length us, event | category | flops | bytes accessed | tf_op | source)
XLA Modules:
  0.0 158.1 jit_solution(6207731791459882128)
XLA Ops:
  0.6 127.1 %chain.1 = (bf16[32,2560]{1,0:T(8,128)(2,1)}, bf16[32,2560]{1,0:T(8,128)(2,1)}, f32[2,2,2560]{2,1,0:T(2,128)}, f32[2,4,2560]{2,1,0:T(4,128)}, f32[2,2560]{1,0:T(...) custom-call(bf16[1,32,2560]{2,1,0:T(8,128)(2,1)} %x_ref.1, ...), custom_call_target="tpu_custom_call" | custom-call | tf_op jit(solution)/shard_map/chain/pallas_call | solution.py:585
  127.7 30.4 %grads.1 = (bf16[32,2560]{1,0:T(8,128)(2,1)}, bf16[32,2560]{1,0:T(8,128)(2,1)}, f32[2,4,2560]{2,1,0:T(4,128)}, f32[2,2,2560]{2,1,0:T(2,128)}, bf16[2,15,2560,128...) custom-call(bf16[32,2560]{1,0:T(8,128)(2,1)} %get-tuple-element.31.y, ...), custom_call_target="tpu_custom_call" | custom-call | tf_op jit(solution)/shard_map/grads/pallas_call | solution.py:612

commit v6 on v5

--- a/solution.py
+++ b/solution.py
@@ -262,6 +262,11 @@
         lnp = ln_ref[layer]
         h_g[layer, me] = normed(res[...], lnp[0:1], lnp[1:2], xh1, rs1, layer)
         ag_start(h_g, layer)
+
+        @pl.when(first)
+        def _():
+            dm_g[N_LAYERS - 1, me] = dy_ref[0]
+            ag_start(dm_g, N_LAYERS - 1, 1)
         acc[...] = jnp.zeros_like(acc)
         wait_w(0, layer)
 
@@ -280,8 +285,6 @@
         @pl.when(first)
         def _():
             load_w(0, 1)
-            dm_g[N_LAYERS - 1, me] = dy_ref[0]
-            ag_start(dm_g, N_LAYERS - 1, 1)
 
         for j in range(3 * HEADS):
             qkv[layer, :, j * HD:(j + 1) * HD] = acc[:, j * HD:(j + 1) * HD].astype(BF16)
@@ -368,6 +371,8 @@
         def _():
             dm_g[0, me] = dres[...].astype(BF16)
             ag_start(dm_g, 0)
+            small_start(0, N_LAYERS - 1)
+            small_start(1, N_LAYERS - 1)
             acct[...] = jnp.zeros_like(acct)
             wait_w(3, 0)
             ag_consume(dm_g, 0, dact_chunk)
@@ -382,8 +387,6 @@
 
         @pl.when(low)
         def _():
-            small_start(0, N_LAYERS - 1)
-            small_start(1, N_LAYERS - 1)
             wait_w(2, 0)
         rs_send(0, lambda c: mm_nt(wu[chunk(c), :], dpre[layer]).T)
 
@@ -403,6 +406,14 @@
         sg2[layer, 2:3, :] = jnp.sum(dres[...], axis=0, keepdims=True)
         da_g[layer, me] = dres[...].astype(BF16)
         ag_start(da_g, layer)
+
+        @pl.when(top)
+        def _():
+            rs_cross(2)
+
+        @pl.when(low)
+        def _():
+            small_start(1, 0)
         acct[0:ATT, :] = jnp.zeros((ATT, SEQ), F32)
 
         @pl.when(low)
@@ -418,11 +429,6 @@
         @pl.when(top)
         def _():
             load_w(1, 0)
-            rs_cross(2)
-
-        @pl.when(low)
-        def _():
-            small_start(1, 0)
 
         for hd in range(HEADS):
             q = qkv[layer, :, hd * HD:(hd + 1) * HD]

time: 158 us -> 159 us (level)
  no operation moved by 1% of the time
where the time goes in v6:
time: 159 us
  Pallas kernels  158 us (99%)
    pallas_call x1, Pallas kernels, device_step(): pl.pallas_call(chain_kernel, name='chain', out_shape=(sds((BLK, D), BF16)...  128 us
    pallas_call x1, Pallas kernels, device_step(): pl.pallas_call(grads_kernel, name='grads', out_shape=(sds((BLK, D), BF16)...  30.4 us

profile of v6, /device:TPU:0, one launch (start us, length us, event | category | flops | bytes accessed | tf_op | source)
XLA Modules:
  0.0 159.2 jit_solution(15780461142097355543)
XLA Ops:
  0.6 128.1 %chain.1 = (bf16[32,2560]{1,0:T(8,128)(2,1)}, bf16[32,2560]{1,0:T(8,128)(2,1)}, f32[2,2,2560]{2,1,0:T(2,128)}, f32[2,4,2560]{2,1,0:T(4,128)}, f32[2,2560]{1,0:T(...) custom-call(bf16[1,32,2560]{2,1,0:T(8,128)(2,1)} %x_ref.1, ...), custom_call_target="tpu_custom_call" | custom-call | tf_op jit(solution)/shard_map/chain/pallas_call | solution.py:591
  128.8 30.4 %grads.1 = (bf16[32,2560]{1,0:T(8,128)(2,1)}, bf16[32,2560]{1,0:T(8,128)(2,1)}, f32[2,4,2560]{2,1,0:T(4,128)}, f32[2,2,2560]{2,1,0:T(2,128)}, bf16[2,15,2560,128...) custom-call(bf16[32,2560]{1,0:T(8,128)(2,1)} %get-tuple-element.31.y, ...), custom_call_target="tpu_custom_call" | custom-call | tf_op jit(solution)/shard_map/grads/pallas_call | solution.py:618

commit v7 on v5

--- a/solution.py
+++ b/solution.py
@@ -368,6 +368,8 @@
         def _():
             dm_g[0, me] = dres[...].astype(BF16)
             ag_start(dm_g, 0)
+            small_start(0, N_LAYERS - 1)
+            small_start(1, N_LAYERS - 1)
             acct[...] = jnp.zeros_like(acct)
             wait_w(3, 0)
             ag_consume(dm_g, 0, dact_chunk)
@@ -382,8 +384,6 @@
 
         @pl.when(low)
         def _():
-            small_start(0, N_LAYERS - 1)
-            small_start(1, N_LAYERS - 1)
             wait_w(2, 0)
         rs_send(0, lambda c: mm_nt(wu[chunk(c), :], dpre[layer]).T)
 

time: 158 us -> 158 us (level)
  no operation moved by 1% of the time
where the time goes in v7:
time: 158 us
  Pallas kernels  158 us (100%)
    pallas_call x1, Pallas kernels, device_step(): pl.pallas_call(chain_kernel, name='chain', out_shape=(sds((BLK, D), BF16)...  127 us
    pallas_call x1, Pallas kernels, device_step(): pl.pallas_call(grads_kernel, name='grads', out_shape=(sds((BLK, D), BF16)...  30.4 us

profile of v7, /device:TPU:0, one launch (start us, length us, event | category | flops | bytes accessed | tf_op | source)
XLA Modules:
  0.0 158.2 jit_solution(4876273560092546687)
XLA Ops:
  0.6 127.1 %chain.1 = (bf16[32,2560]{1,0:T(8,128)(2,1)}, bf16[32,2560]{1,0:T(8,128)(2,1)}, f32[2,2,2560]{2,1,0:T(2,128)}, f32[2,4,2560]{2,1,0:T(4,128)}, f32[2,2560]{1,0:T(...) custom-call(bf16[1,32,2560]{2,1,0:T(8,128)(2,1)} %x_ref.1, ...), custom_call_target="tpu_custom_call" | custom-call | tf_op jit(solution)/shard_map/chain/pallas_call | solution.py:585
  127.8 30.4 %grads.1 = (bf16[32,2560]{1,0:T(8,128)(2,1)}, bf16[32,2560]{1,0:T(8,128)(2,1)}, f32[2,4,2560]{2,1,0:T(4,128)}, f32[2,2,2560]{2,1,0:T(2,128)}, bf16[2,15,2560,128...) custom-call(bf16[32,2560]{1,0:T(8,128)(2,1)} %get-tuple-element.31.y, ...), custom_call_target="tpu_custom_call" | custom-call | tf_op jit(solution)/shard_map/grads/pallas_call | solution.py:612
